TPU v7x, 32 devices: a whole 2x2x4 slice. The times are simulated.
32 devices in a mesh: parts: 2 (over y), brick: 4 (over z), rep: 2 (over x), sub: 2 (over core).
Axes of the slice: x: 2, y: 2, z: 4, core: 2. Of those that a mesh axis runs over, the one named last changes fastest.
Arguments:
- fine_cells: int32 [5, 32768], P(None, ('parts', 'brick', 'rep', 'sub')), parts along dimension 1, may hold values from 0 to 511, as said below
- fine_exponent: float32 [32768], P(('parts', 'brick', 'rep', 'sub')), parts along dimension 0, may hold values from 0.05 to 0.6
- fine_charge: float32 [32768], P(('parts', 'brick', 'rep', 'sub')), parts along dimension 0, may hold values from -6 to 6
- fine_offset: float32 [3, 32768], P(None, ('parts', 'brick', 'rep', 'sub')), parts along dimension 1, may hold values from 0 to 1
- wide_cells: int32 [5, 4096], P(None, ('parts', 'brick', 'rep', 'sub')), parts along dimension 1, may hold values from 0 to 127, as said below
- wide_exponent: float32 [4096], P(('parts', 'brick', 'rep', 'sub')), parts along dimension 0, may hold values from 0.05 to 0.6
- wide_charge: float32 [4096], P(('parts', 'brick', 'rep', 'sub')), parts along dimension 0, may hold values from -6 to 6
- wide_offset: float32 [3, 4096], P(None, ('parts', 'brick', 'rep', 'sub')), parts along dimension 1, may hold values from 0 to 1
Outputs:
- finest_grid: float32 [256, 512, 512], P(('parts', 'brick'), ('rep', 'sub')), parts along dimension 0
- second_grid: float32 [128, 256, 256], P(('parts', 'brick'), ('rep', 'sub')), parts along dimension 0
- middle_grid: float32 [64, 16384], P('parts', 'brick'), parts along dimension 0
- coarse_grid: float32 [32, 4096], P('parts', 'brick'), parts along dimension 0
- coarsest_grid: float32 [16, 1024], P('parts', 'brick'), parts along dimension 0
There are 2 independent parts, one for each index of `parts`. A program takes and returns all parts, laid end to end along the dimension named above; each array names one. Nothing has to cross between parts.
Inputs may be any that keep to these rules, and one draw needn't show every extreme that they name: `fine_cells`: column n is one fine Gaussian: row 0 its level L (0 or 1), row 1 its radius (1 to 4, equal to 4 on every 16th column), rows 2 to 4 its centre cell on level L's grid. The centre lies in the block of the device that holds column n: along the first dimension within that device's brick block of 128/2^L/4 cells, along the second within its block of 512/2^L/4 cells along rep+sub, anywhere along the third. `wide_cells`: column n is one wide Gaussian: row 0 its level L (2 to 4), row 1 its radius (1 to 4, equal to 4 on every 16th column), rows 2 to 4 its centre cell, anywhere on level L's grid.
All inputs are finite; a program needn't handle non-finite values.
Results may differ from a plain program's by a relative error of at most 0.0038.
Values sent between devices are 32-bit elements; how exact they have to be, the bound alone decides.
No kernel may reach another device: no remote copies, remote signals or barrier semaphores. Data moves between devices by JAX's collectives and lax.ppermute only.
A program may use at most 64 MiB of HBM per device.

v0:
```python
import math

import jax
import jax.numpy as jnp
from jax import lax
from jax.sharding import PartitionSpec as P

GRID = 512
ROWS = 128
HALF = 4


def shifted(array, axis, by):
    devices = lax.axis_size(axis)
    pairs = [(i, i + by) for i in range(devices) if 0 <= i + by < devices]
    return lax.ppermute(array, axis, pairs)


def shifted_2(array, axis, by):
    devices = lax.axis_size(axis)
    return lax.ppermute(array, axis, [(i, (i + by) % devices) for i in range(devices)])


def one_factor(offsets, radius, exponent, centre_shift):
    inside = jnp.abs(offsets) <= radius[:, None]
    spread = offsets.astype(jnp.float32) - centre_shift[:, None]
    return jnp.where(inside, jnp.exp(-exponent[:, None] * spread * spread), 0.0)


def wrapped(positions, anchor, period):
    return jnp.mod(positions[None, :] - anchor[:, None] + period // 2, period) - period // 2


def collocate(slot_table, exponent, charge, offset, level_index, row_cells, col_cells, period):
    slot_count = slot_table.shape[1]
    plane_cells = row_cells.shape[0] * col_cells.shape[0]
    target = max(8, 262144 // plane_cells)
    block_size = math.gcd(slot_count, 1 << target.bit_length() - 1)
    depth_cells = jnp.arange(period, dtype=jnp.int32)

    def add_block(block_index, running):
        first_slot = block_index * block_size
        part_table = lax.dynamic_slice_in_dim(slot_table, first_slot, block_size, 1)
        part_exponent = lax.dynamic_slice_in_dim(exponent, first_slot, block_size, 0)
        part_charge = lax.dynamic_slice_in_dim(charge, first_slot, block_size, 0)
        part_offset = lax.dynamic_slice_in_dim(offset, first_slot, block_size, 1)
        radius = part_table[1]
        masked = jnp.where(part_table[0] == level_index, part_charge, 0.0)
        row_factor = one_factor(
            row_cells[None, :] - part_table[2][:, None], radius, part_exponent, part_offset[0]
        )
        col_factor = one_factor(
            wrapped(col_cells, part_table[3], period), radius, part_exponent, part_offset[1]
        )
        depth_factor = one_factor(
            wrapped(depth_cells, part_table[4], period), radius, part_exponent, part_offset[2]
        )
        plane_weight = ((masked[:, None] * row_factor)[:, :, None] * col_factor[:, None, :]).astype(
            jnp.bfloat16
        )
        plane_weight = plane_weight.reshape(block_size, plane_cells)
        depth_weight = depth_factor.astype(jnp.bfloat16)
        return running + lax.dot_general(
            plane_weight, depth_weight, (((0,), (0,)), ((), ())), preferred_element_type=jnp.float32
        )

    start_grid = jnp.zeros((plane_cells, period), jnp.float32)
    running = lax.fori_loop(0, slot_count // block_size, add_block, start_grid)
    return running.reshape(row_cells.shape[0], col_cells.shape[0], period)


def add_rims(tile_part, from_below, from_above, axis_dim):
    inner_count = tile_part.shape[axis_dim] - 2 * HALF
    interior = lax.slice_in_dim(tile_part, HALF, HALF + inner_count, axis=axis_dim)
    lower_widths = [(0, 0), (0, 0), (0, 0)]
    lower_widths[axis_dim] = (0, inner_count - HALF)
    upper_widths = [(0, 0), (0, 0), (0, 0)]
    upper_widths[axis_dim] = (inner_count - HALF, 0)
    return interior + jnp.pad(from_below, lower_widths) + jnp.pad(from_above, upper_widths)


def fold_rows(first_tile, second_tile):
    from_below = shifted(
        (first_tile[first_tile.shape[0] - HALF :], second_tile[second_tile.shape[0] - HALF :]),
        "brick",
        1,
    )
    from_above = shifted((first_tile[:HALF], second_tile[:HALF]), "brick", -1)
    return (
        add_rims(first_tile, from_below[0], from_above[0], 0),
        add_rims(second_tile, from_below[1], from_above[1], 0),
    )


def fold_columns(first_tile, second_tile):
    from_below = shifted_2(
        (
            first_tile[:, first_tile.shape[1] - HALF :],
            second_tile[:, second_tile.shape[1] - HALF :],
        ),
        ("rep", "sub"),
        1,
    )
    from_above = shifted_2((first_tile[:, :HALF], second_tile[:, :HALF]), ("rep", "sub"), -1)
    return (
        add_rims(first_tile, from_below[0], from_above[0], 1),
        add_rims(second_tile, from_below[1], from_above[1], 1),
    )


def per_device(
    fine_cells,
    fine_exponent,
    fine_charge,
    fine_offset,
    wide_cells,
    wide_exponent,
    wide_charge,
    wide_offset,
):
    brick_count = lax.axis_size("brick")
    column_count = lax.axis_size(("rep", "sub"))
    brick_index = lax.axis_index("brick")
    column_index = lax.axis_index(("rep", "sub"))
    tiles = []
    for level_index in range(2):
        row_tile = (ROWS >> level_index) // brick_count
        period = GRID >> level_index
        col_tile = period // column_count
        row_cells = brick_index * row_tile - HALF + jnp.arange(row_tile + 2 * HALF, dtype=jnp.int32)
        col_cells = (
            column_index * col_tile - HALF + jnp.arange(col_tile + 2 * HALF, dtype=jnp.int32)
        )
        tiles.append(
            collocate(
                fine_cells,
                fine_exponent,
                fine_charge,
                fine_offset,
                level_index,
                row_cells,
                col_cells,
                period,
            )
        )
    gathered_ids = lax.all_gather(wide_cells, "brick", axis=1, tiled=True)
    packed = jnp.concatenate([wide_offset, wide_exponent[None, :], wide_charge[None, :]], 0)
    gathered_values = lax.all_gather(packed, "brick", axis=1, tiled=True)
    local_shares = []
    for level_index in range(2, 5):
        rows_here = ROWS >> level_index
        period = GRID >> level_index
        share_width = period * period // brick_count
        first_flat = brick_index * share_width
        first_column = first_flat // period
        column_span = min(period, (share_width + period - 1) // period + 1)
        col_cells = first_column + jnp.arange(column_span, dtype=jnp.int32)
        level_grid = collocate(
            gathered_ids,
            gathered_values[3],
            gathered_values[4],
            gathered_values[0:3],
            level_index,
            jnp.arange(rows_here, dtype=jnp.int32),
            col_cells,
            period,
        )
        level_flat = level_grid.reshape(rows_here, column_span * period)
        local_shares.append(
            lax.dynamic_slice_in_dim(level_flat, first_flat - first_column * period, share_width, 1)
        )
    row_folded = fold_rows(tiles[0], tiles[1])
    folded = fold_columns(row_folded[0], row_folded[1])
    shares = lax.psum((local_shares[0], local_shares[1], local_shares[2]), ("rep", "sub"))
    return (folded[0], folded[1], shares[0], shares[1], shares[2])


def solution(mesh):
    return jax.shard_map(
        per_device,
        mesh=mesh,
        in_specs=(
            P(None, ("parts", "brick", "rep", "sub")),
            P(("parts", "brick", "rep", "sub")),
            P(("parts", "brick", "rep", "sub")),
            P(None, ("parts", "brick", "rep", "sub")),
            P(None, ("parts", "brick", "rep", "sub")),
            P(("parts", "brick", "rep", "sub")),
            P(("parts", "brick", "rep", "sub")),
            P(None, ("parts", "brick", "rep", "sub")),
        ),
        out_specs=(
            P(("parts", "brick"), ("rep", "sub"), None),
            P(("parts", "brick"), ("rep", "sub"), None),
            P("parts", "brick"),
            P("parts", "brick"),
            P("parts", "brick"),
        ),
        check_vma=False,
    )
```

profile of v0, /device:TPU:0, one launch (start us, length us, event | category | flops | bytes accessed | tf_op | source)
XLA Modules:
  0.0 573.9 jit_solution(4575472084314397694)
XLA Ops:
  7.2 426.8 %while.61 = (s32[]{:T(128)}, f32[5440,512]{1,0:T(8,128)}, s32[5,1024]{1,0:T(8,128)}, f32[1024]{0:T(1024)}, f32[1024]{0:T(1024)}, /*index=5*/f32[3,1024]{1,0:T(4,...) while((s32[]{:T(128)}, f32[5440,512]{1,0:T(8,128)}, ...), condition=%wide.region_1.2_spmd.clone, body=%wide.region_0.1_spmd.clone.sunk | while | flops 184640272 | bytes 23727688 | solution.py:68
  10.6 5.9 %select_add_fusion.2 = f32[5440,512]{1,0:T(8,128)} fusion(f32[5440,512]{1,0:T(8,128)} %get-tuple-element.1223, bf16[32,5440]{1,0:T(8,128)(2,1)S(1)} %convert_element_type.392, pred[]{:T(512)S(6)} %compare.45, f32[32]{0:T(128)S(1)} %get-tuple-element.1175, f32[32]{0:T(128)S(1)} %get-tuple-element.1169, s32[32]{0:T(128)S(1)} %get-tuple-element.1170, ...), kind=kOutput, calls=%fused_computation.9.clone.1 | convolution fusion | flops 184188928 | bytes 22630912 | tf_op jit(solution)/shard_map/while/body/eval_jaxpr/dot_general | solution.py:63
  19.9 10.1 %select_add_fusion.2 = f32[5440,512]{1,0:T(8,128)} fusion(f32[5440,512]{1,0:T(8,128)} %get-tuple-element.1223, bf16[32,5440]{1,0:T(8,128)(2,1)S(1)} %convert_element_type.392, pred[]{:T(512)S(6)} %compare.45, f32[32]{0:T(128)S(1)} %get-tuple-element.1175, f32[32]{0:T(128)S(1)} %get-tuple-element.1169, s32[32]{0:T(128)S(1)} %get-tuple-element.1170, ...), kind=kOutput, calls=%fused_computation.9.clone.1 | convolution fusion | flops 184188928 | bytes 22630912 | tf_op jit(solution)/shard_map/while/body/eval_jaxpr/dot_general | solution.py:63
  33.4 10.1 %select_add_fusion.2 = f32[5440,512]{1,0:T(8,128)} fusion(f32[5440,512]{1,0:T(8,128)} %get-tuple-element.1223, bf16[32,5440]{1,0:T(8,128)(2,1)S(1)} %convert_element_type.392, pred[]{:T(512)S(6)} %compare.45, f32[32]{0:T(128)S(1)} %get-tuple-element.1175, f32[32]{0:T(128)S(1)} %get-tuple-element.1169, s32[32]{0:T(128)S(1)} %get-tuple-element.1170, ...), kind=kOutput, calls=%fused_computation.9.clone.1 | convolution fusion | flops 184188928 | bytes 22630912 | tf_op jit(solution)/shard_map/while/body/eval_jaxpr/dot_general | solution.py:63
  46.9 10.1 %select_add_fusion.2 = f32[5440,512]{1,0:T(8,128)} fusion(f32[5440,512]{1,0:T(8,128)} %get-tuple-element.1223, bf16[32,5440]{1,0:T(8,128)(2,1)S(1)} %convert_element_type.392, pred[]{:T(512)S(6)} %compare.45, f32[32]{0:T(128)S(1)} %get-tuple-element.1175, f32[32]{0:T(128)S(1)} %get-tuple-element.1169, s32[32]{0:T(128)S(1)} %get-tuple-element.1170, ...), kind=kOutput, calls=%fused_computation.9.clone.1 | convolution fusion | flops 184188928 | bytes 22630912 | tf_op jit(solution)/shard_map/while/body/eval_jaxpr/dot_general | solution.py:63
  60.3 10.1 %select_add_fusion.2 = f32[5440,512]{1,0:T(8,128)} fusion(f32[5440,512]{1,0:T(8,128)} %get-tuple-element.1223, bf16[32,5440]{1,0:T(8,128)(2,1)S(1)} %convert_element_type.392, pred[]{:T(512)S(6)} %compare.45, f32[32]{0:T(128)S(1)} %get-tuple-element.1175, f32[32]{0:T(128)S(1)} %get-tuple-element.1169, s32[32]{0:T(128)S(1)} %get-tuple-element.1170, ...), kind=kOutput, calls=%fused_computation.9.clone.1 | convolution fusion | flops 184188928 | bytes 22630912 | tf_op jit(solution)/shard_map/while/body/eval_jaxpr/dot_general | solution.py:63
  73.8 10.1 %select_add_fusion.2 = f32[5440,512]{1,0:T(8,128)} fusion(f32[5440,512]{1,0:T(8,128)} %get-tuple-element.1223, bf16[32,5440]{1,0:T(8,128)(2,1)S(1)} %convert_element_type.392, pred[]{:T(512)S(6)} %compare.45, f32[32]{0:T(128)S(1)} %get-tuple-element.1175, f32[32]{0:T(128)S(1)} %get-tuple-element.1169, s32[32]{0:T(128)S(1)} %get-tuple-element.1170, ...), kind=kOutput, calls=%fused_computation.9.clone.1 | convolution fusion | flops 184188928 | bytes 22630912 | tf_op jit(solution)/shard_map/while/body/eval_jaxpr/dot_general | solution.py:63
  87.3 10.1 %select_add_fusion.2 = f32[5440,512]{1,0:T(8,128)} fusion(f32[5440,512]{1,0:T(8,128)} %get-tuple-element.1223, bf16[32,5440]{1,0:T(8,128)(2,1)S(1)} %convert_element_type.392, pred[]{:T(512)S(6)} %compare.45, f32[32]{0:T(128)S(1)} %get-tuple-element.1175, f32[32]{0:T(128)S(1)} %get-tuple-element.1169, s32[32]{0:T(128)S(1)} %get-tuple-element.1170, ...), kind=kOutput, calls=%fused_computation.9.clone.1 | convolution fusion | flops 184188928 | bytes 22630912 | tf_op jit(solution)/shard_map/while/body/eval_jaxpr/dot_general | solution.py:63
  100.7 10.1 %select_add_fusion.2 = f32[5440,512]{1,0:T(8,128)} fusion(f32[5440,512]{1,0:T(8,128)} %get-tuple-element.1223, bf16[32,5440]{1,0:T(8,128)(2,1)S(1)} %convert_element_type.392, pred[]{:T(512)S(6)} %compare.45, f32[32]{0:T(128)S(1)} %get-tuple-element.1175, f32[32]{0:T(128)S(1)} %get-tuple-element.1169, s32[32]{0:T(128)S(1)} %get-tuple-element.1170, ...), kind=kOutput, calls=%fused_computation.9.clone.1 | convolution fusion | flops 184188928 | bytes 22630912 | tf_op jit(solution)/shard_map/while/body/eval_jaxpr/dot_general | solution.py:63
  114.2 10.1 %select_add_fusion.2 = f32[5440,512]{1,0:T(8,128)} fusion(f32[5440,512]{1,0:T(8,128)} %get-tuple-element.1223, bf16[32,5440]{1,0:T(8,128)(2,1)S(1)} %convert_element_type.392, pred[]{:T(512)S(6)} %compare.45, f32[32]{0:T(128)S(1)} %get-tuple-element.1175, f32[32]{0:T(128)S(1)} %get-tuple-element.1169, s32[32]{0:T(128)S(1)} %get-tuple-element.1170, ...), kind=kOutput, calls=%fused_computation.9.clone.1 | convolution fusion | flops 184188928 | bytes 22630912 | tf_op jit(solution)/shard_map/while/body/eval_jaxpr/dot_general | solution.py:63
  127.7 10.1 %select_add_fusion.2 = f32[5440,512]{1,0:T(8,128)} fusion(f32[5440,512]{1,0:T(8,128)} %get-tuple-element.1223, bf16[32,5440]{1,0:T(8,128)(2,1)S(1)} %convert_element_type.392, pred[]{:T(512)S(6)} %compare.45, f32[32]{0:T(128)S(1)} %get-tuple-element.1175, f32[32]{0:T(128)S(1)} %get-tuple-element.1169, s32[32]{0:T(128)S(1)} %get-tuple-element.1170, ...), kind=kOutput, calls=%fused_computation.9.clone.1 | convolution fusion | flops 184188928 | bytes 22630912 | tf_op jit(solution)/shard_map/while/body/eval_jaxpr/dot_general | solution.py:63
  141.1 10.1 %select_add_fusion.2 = f32[5440,512]{1,0:T(8,128)} fusion(f32[5440,512]{1,0:T(8,128)} %get-tuple-element.1223, bf16[32,5440]{1,0:T(8,128)(2,1)S(1)} %convert_element_type.392, pred[]{:T(512)S(6)} %compare.45, f32[32]{0:T(128)S(1)} %get-tuple-element.1175, f32[32]{0:T(128)S(1)} %get-tuple-element.1169, s32[32]{0:T(128)S(1)} %get-tuple-element.1170, ...), kind=kOutput, calls=%fused_computation.9.clone.1 | convolution fusion | flops 184188928 | bytes 22630912 | tf_op jit(solution)/shard_map/while/body/eval_jaxpr/dot_general | solution.py:63
  154.6 10.1 %select_add_fusion.2 = f32[5440,512]{1,0:T(8,128)} fusion(f32[5440,512]{1,0:T(8,128)} %get-tuple-element.1223, bf16[32,5440]{1,0:T(8,128)(2,1)S(1)} %convert_element_type.392, pred[]{:T(512)S(6)} %compare.45, f32[32]{0:T(128)S(1)} %get-tuple-element.1175, f32[32]{0:T(128)S(1)} %get-tuple-element.1169, s32[32]{0:T(128)S(1)} %get-tuple-element.1170, ...), kind=kOutput, calls=%fused_computation.9.clone.1 | convolution fusion | flops 184188928 | bytes 22630912 | tf_op jit(solution)/shard_map/while/body/eval_jaxpr/dot_general | solution.py:63
  168.1 10.1 %select_add_fusion.2 = f32[5440,512]{1,0:T(8,128)} fusion(f32[5440,512]{1,0:T(8,128)} %get-tuple-element.1223, bf16[32,5440]{1,0:T(8,128)(2,1)S(1)} %convert_element_type.392, pred[]{:T(512)S(6)} %compare.45, f32[32]{0:T(128)S(1)} %get-tuple-element.1175, f32[32]{0:T(128)S(1)} %get-tuple-element.1169, s32[32]{0:T(128)S(1)} %get-tuple-element.1170, ...), kind=kOutput, calls=%fused_computation.9.clone.1 | convolution fusion | flops 184188928 | bytes 22630912 | tf_op jit(solution)/shard_map/while/body/eval_jaxpr/dot_general | solution.py:63
  181.5 10.1 %select_add_fusion.2 = f32[5440,512]{1,0:T(8,128)} fusion(f32[5440,512]{1,0:T(8,128)} %get-tuple-element.1223, bf16[32,5440]{1,0:T(8,128)(2,1)S(1)} %convert_element_type.392, pred[]{:T(512)S(6)} %compare.45, f32[32]{0:T(128)S(1)} %get-tuple-element.1175, f32[32]{0:T(128)S(1)} %get-tuple-element.1169, s32[32]{0:T(128)S(1)} %get-tuple-element.1170, ...), kind=kOutput, calls=%fused_computation.9.clone.1 | convolution fusion | flops 184188928 | bytes 22630912 | tf_op jit(solution)/shard_map/while/body/eval_jaxpr/dot_general | solution.py:63
  195.0 10.1 %select_add_fusion.2 = f32[5440,512]{1,0:T(8,128)} fusion(f32[5440,512]{1,0:T(8,128)} %get-tuple-element.1223, bf16[32,5440]{1,0:T(8,128)(2,1)S(1)} %convert_element_type.392, pred[]{:T(512)S(6)} %compare.45, f32[32]{0:T(128)S(1)} %get-tuple-element.1175, f32[32]{0:T(128)S(1)} %get-tuple-element.1169, s32[32]{0:T(128)S(1)} %get-tuple-element.1170, ...), kind=kOutput, calls=%fused_computation.9.clone.1 | convolution fusion | flops 184188928 | bytes 22630912 | tf_op jit(solution)/shard_map/while/body/eval_jaxpr/dot_general | solution.py:63
  208.5 10.1 %select_add_fusion.2 = f32[5440,512]{1,0:T(8,128)} fusion(f32[5440,512]{1,0:T(8,128)} %get-tuple-element.1223, bf16[32,5440]{1,0:T(8,128)(2,1)S(1)} %convert_element_type.392, pred[]{:T(512)S(6)} %compare.45, f32[32]{0:T(128)S(1)} %get-tuple-element.1175, f32[32]{0:T(128)S(1)} %get-tuple-element.1169, s32[32]{0:T(128)S(1)} %get-tuple-element.1170, ...), kind=kOutput, calls=%fused_computation.9.clone.1 | convolution fusion | flops 184188928 | bytes 22630912 | tf_op jit(solution)/shard_map/while/body/eval_jaxpr/dot_general | solution.py:63
  221.9 10.1 %select_add_fusion.2 = f32[5440,512]{1,0:T(8,128)} fusion(f32[5440,512]{1,0:T(8,128)} %get-tuple-element.1223, bf16[32,5440]{1,0:T(8,128)(2,1)S(1)} %convert_element_type.392, pred[]{:T(512)S(6)} %compare.45, f32[32]{0:T(128)S(1)} %get-tuple-element.1175, f32[32]{0:T(128)S(1)} %get-tuple-element.1169, s32[32]{0:T(128)S(1)} %get-tuple-element.1170, ...), kind=kOutput, calls=%fused_computation.9.clone.1 | convolution fusion | flops 184188928 | bytes 22630912 | tf_op jit(solution)/shard_map/while/body/eval_jaxpr/dot_general | solution.py:63
  235.4 10.1 %select_add_fusion.2 = f32[5440,512]{1,0:T(8,128)} fusion(f32[5440,512]{1,0:T(8,128)} %get-tuple-element.1223, bf16[32,5440]{1,0:T(8,128)(2,1)S(1)} %convert_element_type.392, pred[]{:T(512)S(6)} %compare.45, f32[32]{0:T(128)S(1)} %get-tuple-element.1175, f32[32]{0:T(128)S(1)} %get-tuple-element.1169, s32[32]{0:T(128)S(1)} %get-tuple-element.1170, ...), kind=kOutput, calls=%fused_computation.9.clone.1 | convolution fusion | flops 184188928 | bytes 22630912 | tf_op jit(solution)/shard_map/while/body/eval_jaxpr/dot_general | solution.py:63
  248.9 10.1 %select_add_fusion.2 = f32[5440,512]{1,0:T(8,128)} fusion(f32[5440,512]{1,0:T(8,128)} %get-tuple-element.1223, bf16[32,5440]{1,0:T(8,128)(2,1)S(1)} %convert_element_type.392, pred[]{:T(512)S(6)} %compare.45, f32[32]{0:T(128)S(1)} %get-tuple-element.1175, f32[32]{0:T(128)S(1)} %get-tuple-element.1169, s32[32]{0:T(128)S(1)} %get-tuple-element.1170, ...), kind=kOutput, calls=%fused_computation.9.clone.1 | convolution fusion | flops 184188928 | bytes 22630912 | tf_op jit(solution)/shard_map/while/body/eval_jaxpr/dot_general | solution.py:63
  262.3 10.1 %select_add_fusion.2 = f32[5440,512]{1,0:T(8,128)} fusion(f32[5440,512]{1,0:T(8,128)} %get-tuple-element.1223, bf16[32,5440]{1,0:T(8,128)(2,1)S(1)} %convert_element_type.392, pred[]{:T(512)S(6)} %compare.45, f32[32]{0:T(128)S(1)} %get-tuple-element.1175, f32[32]{0:T(128)S(1)} %get-tuple-element.1169, s32[32]{0:T(128)S(1)} %get-tuple-element.1170, ...), kind=kOutput, calls=%fused_computation.9.clone.1 | convolution fusion | flops 184188928 | bytes 22630912 | tf_op jit(solution)/shard_map/while/body/eval_jaxpr/dot_general | solution.py:63
  275.8 10.1 %select_add_fusion.2 = f32[5440,512]{1,0:T(8,128)} fusion(f32[5440,512]{1,0:T(8,128)} %get-tuple-element.1223, bf16[32,5440]{1,0:T(8,128)(2,1)S(1)} %convert_element_type.392, pred[]{:T(512)S(6)} %compare.45, f32[32]{0:T(128)S(1)} %get-tuple-element.1175, f32[32]{0:T(128)S(1)} %get-tuple-element.1169, s32[32]{0:T(128)S(1)} %get-tuple-element.1170, ...), kind=kOutput, calls=%fused_computation.9.clone.1 | convolution fusion | flops 184188928 | bytes 22630912 | tf_op jit(solution)/shard_map/while/body/eval_jaxpr/dot_general | solution.py:63
  289.3 10.1 %select_add_fusion.2 = f32[5440,512]{1,0:T(8,128)} fusion(f32[5440,512]{1,0:T(8,128)} %get-tuple-element.1223, bf16[32,5440]{1,0:T(8,128)(2,1)S(1)} %convert_element_type.392, pred[]{:T(512)S(6)} %compare.45, f32[32]{0:T(128)S(1)} %get-tuple-element.1175, f32[32]{0:T(128)S(1)} %get-tuple-element.1169, s32[32]{0:T(128)S(1)} %get-tuple-element.1170, ...), kind=kOutput, calls=%fused_computation.9.clone.1 | convolution fusion | flops 184188928 | bytes 22630912 | tf_op jit(solution)/shard_map/while/body/eval_jaxpr/dot_general | solution.py:63
  302.7 10.1 %select_add_fusion.2 = f32[5440,512]{1,0:T(8,128)} fusion(f32[5440,512]{1,0:T(8,128)} %get-tuple-element.1223, bf16[32,5440]{1,0:T(8,128)(2,1)S(1)} %convert_element_type.392, pred[]{:T(512)S(6)} %compare.45, f32[32]{0:T(128)S(1)} %get-tuple-element.1175, f32[32]{0:T(128)S(1)} %get-tuple-element.1169, s32[32]{0:T(128)S(1)} %get-tuple-element.1170, ...), kind=kOutput, calls=%fused_computation.9.clone.1 | convolution fusion | flops 184188928 | bytes 22630912 | tf_op jit(solution)/shard_map/while/body/eval_jaxpr/dot_general | solution.py:63
  316.2 10.1 %select_add_fusion.2 = f32[5440,512]{1,0:T(8,128)} fusion(f32[5440,512]{1,0:T(8,128)} %get-tuple-element.1223, bf16[32,5440]{1,0:T(8,128)(2,1)S(1)} %convert_element_type.392, pred[]{:T(512)S(6)} %compare.45, f32[32]{0:T(128)S(1)} %get-tuple-element.1175, f32[32]{0:T(128)S(1)} %get-tuple-element.1169, s32[32]{0:T(128)S(1)} %get-tuple-element.1170, ...), kind=kOutput, calls=%fused_computation.9.clone.1 | convolution fusion | flops 184188928 | bytes 22630912 | tf_op jit(solution)/shard_map/while/body/eval_jaxpr/dot_general | solution.py:63
  329.7 10.1 %select_add_fusion.2 = f32[5440,512]{1,0:T(8,128)} fusion(f32[5440,512]{1,0:T(8,128)} %get-tuple-element.1223, bf16[32,5440]{1,0:T(8,128)(2,1)S(1)} %convert_element_type.392, pred[]{:T(512)S(6)} %compare.45, f32[32]{0:T(128)S(1)} %get-tuple-element.1175, f32[32]{0:T(128)S(1)} %get-tuple-element.1169, s32[32]{0:T(128)S(1)} %get-tuple-element.1170, ...), kind=kOutput, calls=%fused_computation.9.clone.1 | convolution fusion | flops 184188928 | bytes 22630912 | tf_op jit(solution)/shard_map/while/body/eval_jaxpr/dot_general | solution.py:63
  343.1 10.1 %select_add_fusion.2 = f32[5440,512]{1,0:T(8,128)} fusion(f32[5440,512]{1,0:T(8,128)} %get-tuple-element.1223, bf16[32,5440]{1,0:T(8,128)(2,1)S(1)} %convert_element_type.392, pred[]{:T(512)S(6)} %compare.45, f32[32]{0:T(128)S(1)} %get-tuple-element.1175, f32[32]{0:T(128)S(1)} %get-tuple-element.1169, s32[32]{0:T(128)S(1)} %get-tuple-element.1170, ...), kind=kOutput, calls=%fused_computation.9.clone.1 | convolution fusion | flops 184188928 | bytes 22630912 | tf_op jit(solution)/shard_map/while/body/eval_jaxpr/dot_general | solution.py:63
  356.6 10.1 %select_add_fusion.2 = f32[5440,512]{1,0:T(8,128)} fusion(f32[5440,512]{1,0:T(8,128)} %get-tuple-element.1223, bf16[32,5440]{1,0:T(8,128)(2,1)S(1)} %convert_element_type.392, pred[]{:T(512)S(6)} %compare.45, f32[32]{0:T(128)S(1)} %get-tuple-element.1175, f32[32]{0:T(128)S(1)} %get-tuple-element.1169, s32[32]{0:T(128)S(1)} %get-tuple-element.1170, ...), kind=kOutput, calls=%fused_computation.9.clone.1 | convolution fusion | flops 184188928 | bytes 22630912 | tf_op jit(solution)/shard_map/while/body/eval_jaxpr/dot_general | solution.py:63
  370.1 10.1 %select_add_fusion.2 = f32[5440,512]{1,0:T(8,128)} fusion(f32[5440,512]{1,0:T(8,128)} %get-tuple-element.1223, bf16[32,5440]{1,0:T(8,128)(2,1)S(1)} %convert_element_type.392, pred[]{:T(512)S(6)} %compare.45, f32[32]{0:T(128)S(1)} %get-tuple-element.1175, f32[32]{0:T(128)S(1)} %get-tuple-element.1169, s32[32]{0:T(128)S(1)} %get-tuple-element.1170, ...), kind=kOutput, calls=%fused_computation.9.clone.1 | convolution fusion | flops 184188928 | bytes 22630912 | tf_op jit(solution)/shard_map/while/body/eval_jaxpr/dot_general | solution.py:63
  383.5 10.1 %select_add_fusion.2 = f32[5440,512]{1,0:T(8,128)} fusion(f32[5440,512]{1,0:T(8,128)} %get-tuple-element.1223, bf16[32,5440]{1,0:T(8,128)(2,1)S(1)} %convert_element_type.392, pred[]{:T(512)S(6)} %compare.45, f32[32]{0:T(128)S(1)} %get-tuple-element.1175, f32[32]{0:T(128)S(1)} %get-tuple-element.1169, s32[32]{0:T(128)S(1)} %get-tuple-element.1170, ...), kind=kOutput, calls=%fused_computation.9.clone.1 | convolution fusion | flops 184188928 | bytes 22630912 | tf_op jit(solution)/shard_map/while/body/eval_jaxpr/dot_general | solution.py:63
  397.0 10.1 %select_add_fusion.2 = f32[5440,512]{1,0:T(8,128)} fusion(f32[5440,512]{1,0:T(8,128)} %get-tuple-element.1223, bf16[32,5440]{1,0:T(8,128)(2,1)S(1)} %convert_element_type.392, pred[]{:T(512)S(6)} %compare.45, f32[32]{0:T(128)S(1)} %get-tuple-element.1175, f32[32]{0:T(128)S(1)} %get-tuple-element.1169, s32[32]{0:T(128)S(1)} %get-tuple-element.1170, ...), kind=kOutput, calls=%fused_computation.9.clone.1 | convolution fusion | flops 184188928 | bytes 22630912 | tf_op jit(solution)/shard_map/while/body/eval_jaxpr/dot_general | solution.py:63
  410.5 10.1 %select_add_fusion.2 = f32[5440,512]{1,0:T(8,128)} fusion(f32[5440,512]{1,0:T(8,128)} %get-tuple-element.1223, bf16[32,5440]{1,0:T(8,128)(2,1)S(1)} %convert_element_type.392, pred[]{:T(512)S(6)} %compare.45, f32[32]{0:T(128)S(1)} %get-tuple-element.1175, f32[32]{0:T(128)S(1)} %get-tuple-element.1169, s32[32]{0:T(128)S(1)} %get-tuple-element.1170, ...), kind=kOutput, calls=%fused_computation.9.clone.1 | convolution fusion | flops 184188928 | bytes 22630912 | tf_op jit(solution)/shard_map/while/body/eval_jaxpr/dot_general | solution.py:63
  423.9 10.1 %select_add_fusion.2 = f32[5440,512]{1,0:T(8,128)} fusion(f32[5440,512]{1,0:T(8,128)} %get-tuple-element.1223, bf16[32,5440]{1,0:T(8,128)(2,1)S(1)} %convert_element_type.392, pred[]{:T(512)S(6)} %compare.45, f32[32]{0:T(128)S(1)} %get-tuple-element.1175, f32[32]{0:T(128)S(1)} %get-tuple-element.1169, s32[32]{0:T(128)S(1)} %get-tuple-element.1170, ...), kind=kOutput, calls=%fused_computation.9.clone.1 | convolution fusion | flops 184188928 | bytes 22630912 | tf_op jit(solution)/shard_map/while/body/eval_jaxpr/dot_general | solution.py:63
  434.0 3.1 fusion.178
  437.2 1.3 collective-permute-start.1
  438.5 6.6 %collective-permute-start = (f32[4,136,512]{2,1,0:T(8,128)}, f32[4,136,512]{2,1,0:T(8,128)}, u32[]{:S(2)}, u32[]{:S(2)}) collective-permute-start(f32[4,136,512]{2,1,0:T(8,128)} %bitcast.1), channel_id=1, source_target_pairs={{0,4},{4,8},{8,12},{1,5},{5,9},{9,13},{2,6},{6,10},{10,14},{3,7},{... | collective-permute-start | bytes 3342344 | tf_op jit(solution)/shard_map/ppermute | solution.py:16
  445.1 26.3 %while.62 = (s32[]{:T(128)}, f32[1728,256]{1,0:T(8,128)S(1)}, s32[5,1024]{1,0:T(8,128)}, f32[1024]{0:T(1024)}, f32[1024]{0:T(1024)}, /*index=5*/f32[3,1024]{1,0:...) while((s32[]{:T(128)}, f32[1728,256]{1,0:T(8,128)S(1)}, ...), condition=%wide.region_3.4_spmd.clone, body=%wide.region_2.3_spmd.clone.sunk | while | flops 115515880 | bytes 4547529 | solution.py:68
  457.5 0.8 convolution_add_fusion.4
  460.8 0.8 convolution_add_fusion.4
  464.0 0.8 convolution_add_fusion.4
  467.3 0.8 convolution_add_fusion.4
  470.6 0.8 convolution_add_fusion.4
  471.4 0.8 fusion.180
  472.3 1.3 collective-permute-start.5
  473.5 4.6 collective-permute-start.4
  478.2 14.2 %all_gather.7 = f32[5,512]{1,0:T(8,128)S(1)} all-gather(f32[5,128]{1,0:T(8,128)S(1)} %pad_maximum_fusion), channel_id=1, replica_groups=mesh['parts'=2,'brick'=4,'rep'=2,'sub'=2] {'brick'}, dimensions={1}, use_global_device_ids=true | all-gather | bytes 12800 | tf_op jit(solution)/shard_map/all_gather | solution.py:148
  493.0 13.2 %all_gather.6 = s32[5,512]{1,0:T(8,128)S(1)} all-gather(s32[5,128]{1,0:T(8,128)S(1)} %copy-done.6), channel_id=1, replica_groups=mesh['parts'=2,'brick'=4,'rep'=2,'sub'=2] {'brick'}, dimensions={1}, use_global_device_ids=true | all-gather | bytes 12800 | tf_op jit(solution)/shard_map/all_gather | solution.py:146
  508.0 3.4 while.63
  512.2 0.8 fusion.155
  513.8 0.8 convert_element_type.284
  514.7 1.5 fusion.128
  516.3 0.8 constant_dynamic-slice_fusion.8
  518.7 8.0 %slice.384 = f32[4352,512]{1,0:T(8,128)} slice(f32[5440,512]{1,0:T(8,128)} %get-tuple-element.815), slice={[544:4896], [0:512]} | slice | bytes 17825792 | tf_op jit(solution)/shard_map/slice | solution.py:74
  527.5 1.2 fusion.130
  528.9 6.8 %psum.23 = f32[8,256]{1,0:T(8,128)} all-reduce(f32[8,256]{1,0:T(8,128)S(1)} %constant_dynamic-slice_fusion.6), channel_id=1, replica_groups=mesh['parts'=2,'brick'=4,'rep'=2,'sub'=2] {'rep','sub'}, use_global_device_ids=true, to_apply=%region_8.9 | all-reduce | flops 2048 | bytes 16384 | tf_op jit(solution)/shard_map/psum | solution.py:174
  536.4 9.1 %pad_add_fusion = f32[32,136,512]{2,1,0:T(8,128)} fusion(f32[4,136,512]{2,1,0:T(8,128)} %collective-permute-done.1, f32[32,136,512]{2,1,0:T(8,128)} %bitcast.104, f32[4,136,512]{2,1,0:T(8,128)} %collective-permute-done), kind=kLoop, calls=%fused_computation.189 | loop fusion | flops 4456448 | bytes 20054016 | tf_op jit(solution)/shard_map/add | solution.py:79
  545.5 1.3 fusion.179
  546.8 1.8 collective-permute-start.3
  548.5 1.1 fusion.117
  549.7 6.1 %collective-permute-done.3 = f32[32,4,512]{2,1,0:T(4,128)S(1)} collective-permute-done((f32[32,4,512]{2,1,0:T(4,128)S(1)}, f32[32,4,512]{2,1,0:T(4,128)S(1)}, u32[]{:S(2)}, u32[]{:S(2)}) %collective-permute-start.3) | collective-permute-done | bytes 262176 | tf_op jit(solution)/shard_map/ppermute | solution.py:21
  555.7 1.5 collective-permute-done.2
  557.3 6.5 %fusion.116 = f32[32,128,512]{2,1,0:T(8,128)} fusion(f32[32,136,512]{2,1,0:T(8,128)} %pad_add_fusion, f32[32,4,512]{2,1,0:T(4,128)S(1)} %collective-permute-done.3, f32[32,4,512]{2,1,0:T(4,128)S(1)} %collective-permute-done.2), kind=kLoop, calls=%fused_computation.191 | loop fusion | flops 4194304 | bytes 17301504 | tf_op jit(solution)/shard_map/add | solution.py:79
  563.7 1.9 copy.37
  565.6 1.5 copy.38
  (541 shorter events, 138.4 us)
Async XLA Ops:
  7.2 556.6 %all-reduce.11.cloned.1.call-start = ((), (), s32[]{:S(2)}) async-start(), calls=%async_computation | async-start | bytes 1179648 | tf_op jit(solution)/shard_map/psum | solution.py:174
  437.2 99.2 %collective-permute-start.1 = (f32[4,136,512]{2,1,0:T(8,128)}, f32[4,136,512]{2,1,0:T(8,128)}, u32[]{:S(2)}, u32[]{:S(2)}) collective-permute-start(f32[4,136,512]{2,1,0:T(8,128)} %bitcast.2), channel_id=1, source_target_pairs={{4,0},{8,4},{12,8},{5,1},{9,5},{13,9},{6,2},{10,6},{14,10},{7,3},{... | collective-permute-start | bytes 3342344 | tf_op jit(solution)/shard_map/ppermute | solution.py:16
  438.5 97.9 %collective-permute-start = (f32[4,136,512]{2,1,0:T(8,128)}, f32[4,136,512]{2,1,0:T(8,128)}, u32[]{:S(2)}, u32[]{:S(2)}) collective-permute-start(f32[4,136,512]{2,1,0:T(8,128)} %bitcast.1), channel_id=1, source_target_pairs={{0,4},{4,8},{8,12},{1,5},{5,9},{9,13},{2,6},{6,10},{10,14},{3,7},{... | collective-permute-start | bytes 3342344 | tf_op jit(solution)/shard_map/ppermute | solution.py:16
  445.1 33.0 %copy-start.7 = (f32[3,128]{1,0:T(4,128)S(1)}, f32[3,128]{1,0:T(4,128)}, u32[]{:S(2)}) copy-start(f32[3,128]{1,0:T(4,128)} %param.21) | copy-start | bytes 4612
  445.1 33.0 %copy-start.10 = (f32[128]{0:T(128)S(1)}, f32[128]{0:T(128)}, u32[]{:S(2)}) copy-start(f32[128]{0:T(128)} %param.20) | copy-start | bytes 1540
  445.1 33.0 %copy-start.11 = (f32[128]{0:T(128)S(1)}, f32[128]{0:T(128)}, u32[]{:S(2)}) copy-start(f32[128]{0:T(128)} %param.19) | copy-start | bytes 1540
  445.1 47.9 %copy-start.6 = (s32[5,128]{1,0:T(8,128)S(1)}, s32[5,128]{1,0:T(8,128)}, u32[]{:S(2)}) copy-start(s32[5,128]{1,0:T(8,128)} %param.18) | copy-start | bytes 7684
  472.3 63.4 %collective-permute-start.5 = (f32[4,72,256]{2,1,0:T(8,128)}, f32[4,72,256]{2,1,0:T(8,128)S(1)}, u32[]{:S(2)}, u32[]{:S(2)}) collective-permute-start(f32[4,72,256]{2,1,0:T(8,128)} %bitcast.5), channel_id=1, source_target_pairs={{4,0},{8,4},{12,8},{5,1},{9,5},{13,9},{6,2},{10,6},{14,10},{7,3},{... | collective-permute-start | bytes 884744 | tf_op jit(solution)/shard_map/ppermute | solution.py:16
  473.5 62.1 %collective-permute-start.4 = (f32[4,72,256]{2,1,0:T(8,128)}, f32[4,72,256]{2,1,0:T(8,128)S(1)}, u32[]{:S(2)}, u32[]{:S(2)}) collective-permute-start(f32[4,72,256]{2,1,0:T(8,128)} %bitcast.4), channel_id=1, source_target_pairs={{0,4},{4,8},{8,12},{1,5},{5,9},{9,13},{2,6},{6,10},{10,14},{3,7},{... | collective-permute-start | bytes 884744 | tf_op jit(solution)/shard_map/ppermute | solution.py:16
  506.8 11.8 %copy-start.1 = (s32[1,512]{1,0:T(1,128)}, s32[1,512]{1,0:T(1,128)S(1)}, u32[]{:S(2)}) copy-start(s32[1,512]{1,0:T(1,128)S(1)} %get-tuple-element.1006) | copy-start | bytes 6148
  508.0 10.6 %copy-start = (f32[512]{0:T(512)}, f32[512]{0:T(512)S(1)}, u32[]{:S(2)}) copy-start(f32[512]{0:T(512)S(1)} %neg.57) | copy-start | bytes 6148
  511.4 3.2 copy-start.8
  511.4 3.2 copy-start.9
  514.6 3.3 copy-start.2
  514.6 3.3 copy-start.4
  514.7 4.0 copy-start.3
  514.7 4.0 copy-start.5
  535.8 12.7 %collective-permute-start.7 = (f32[16,4,256]{2,1,0:T(4,128)S(1)}, f32[16,4,256]{2,1,0:T(4,128)S(1)}, u32[]{:S(2)}, u32[]{:S(2)}) collective-permute-start(f32[16,4,256]{2,1,0:T(4,128)S(1)} %get-tuple-element.1003), channel_id=1, source_target_pairs={{0,3},{1,0},{2,1},{3,2},{4,7},{5,4},{6,5},{7,6},{8,11},{9,8},{10,9... | collective-permute-start | bytes 196616 | tf_op jit(solution)/shard_map/ppermute | solution.py:21
  536.3 12.2 %collective-permute-start.6 = (f32[16,4,256]{2,1,0:T(4,128)S(1)}, f32[16,4,256]{2,1,0:T(4,128)S(1)}, u32[]{:S(2)}, u32[]{:S(2)}) collective-permute-start(f32[16,4,256]{2,1,0:T(4,128)S(1)} %get-tuple-element.1002), channel_id=1, source_target_pairs={{0,1},{1,2},{2,3},{3,0},{4,5},{5,6},{6,7},{7,4},{8,9},{9,10},{10,1... | collective-permute-start | bytes 196616 | tf_op jit(solution)/shard_map/ppermute | solution.py:21
  546.8 8.9 %collective-permute-start.3 = (f32[32,4,512]{2,1,0:T(4,128)S(1)}, f32[32,4,512]{2,1,0:T(4,128)S(1)}, u32[]{:S(2)}, u32[]{:S(2)}) collective-permute-start(f32[32,4,512]{2,1,0:T(4,128)S(1)} %get-tuple-element.999), channel_id=1, source_target_pairs={{0,3},{1,0},{2,1},{3,2},{4,7},{5,4},{6,5},{7,6},{8,11},{9,8},{10,9... | collective-permute-start | bytes 786440 | tf_op jit(solution)/shard_map/ppermute | solution.py:21
  548.5 8.7 %collective-permute-start.2 = (f32[32,4,512]{2,1,0:T(4,128)S(1)}, f32[32,4,512]{2,1,0:T(4,128)S(1)}, u32[]{:S(2)}, u32[]{:S(2)}) collective-permute-start(f32[32,4,512]{2,1,0:T(4,128)S(1)} %get-tuple-element.998), channel_id=1, source_target_pairs={{0,1},{1,2},{2,3},{3,0},{4,5},{5,6},{6,7},{7,4},{8,9},{9,10},{10,1... | collective-permute-start | bytes 786440 | tf_op jit(solution)/shard_map/ppermute | solution.py:21
Sparse Core Ops, SparseCore 0:
  518.0 35.4 all-reduce.10
where the time goes:
time: 579 us; the launch traced here: 574 us
  matrix products  330 us (57%)
  local copies, waits for them, and re-layouts  99.8 us (17%)
  other arithmetic  69.8 us (12%)
  blocking collectives  34.2 us (6%)
  starting transfers between devices  16.1 us (3%)
  between operations  14.3 us (2%)
  waiting for transfers between devices  7.63 us (1%)
    dot_general x46, matrix products, add_block(): lax.dot_general(plane_weight, depth_weight, (((0,), (0,)), ((), ())), pre...  330 us
    select_n x45, other arithmetic, add_block(): masked = jnp.where(part_table[0] == level_index, part_charge, 0.0)  32.1 us
    dynamic_slice x44, local copies, waits for them, and re-layouts, add_block(): part_table = lax.dynamic_slice_in_dim(slot_table, first_slot, block_size, 1)  29.8 us
    dynamic_slice x44, local copies, waits for them, and re-layouts, add_block(): part_offset = lax.dynamic_slice_in_dim(offset, first_slot, block_size, 1)  29.6 us
    convert_element_type x38, local copies, waits for them, and re-layouts, add_block(): ((masked[:, None] * row_factor)[:, :, None] * col_factor[:, None, :]).ast...  20.1 us
    add x4, other arithmetic, add_rims(): interior + jnp.pad(from_below, lower_widths)  16.8 us
    all_gather x1, blocking collectives, per_device(): gathered_values = lax.all_gather(packed, 'brick', axis=1, tiled=True)  14.2 us
    ppermute x4, starting transfers between devices, shifted(): return lax.ppermute(array, axis, pairs)  13.8 us
  transfers between devices with their start and end apart: 9, of which 2 were waited for; matrix products, arithmetic and copies ran while one was open for 12% of the time, Pallas kernels for 0%

commit v1 on v0

v1 whole, which is shorter than its diff:
```python
import math

import jax
import jax.numpy as jnp
from jax import lax
from jax.experimental import pallas as pl
from jax.experimental.pallas import tpu as pltpu
from jax.sharding import PartitionSpec as P

GRID = 512
ROWS = 128
HALF = 4
SIDE = 8
COLUMNS = ("rep", "sub")
LEVEL, RADIUS, CENTRE, SHIFT, EXPONENT, CHARGE = 0, 1, 2, 5, 8, 9


def pack(cells, exponent, charge, offset):
    return jnp.concatenate(
        [cells.astype(jnp.float32), offset, exponent[None, :], charge[None, :]], 0
    )


def shifted(array, axis, by, wrap):
    devices = lax.axis_size(axis)
    pairs = [(i, (i + by) % devices) for i in range(devices) if wrap or 0 <= i + by < devices]
    return lax.ppermute(array, axis, pairs)


def window(first, count, table, dim, period):
    radius = table(RADIUS)
    span = radius.astype(jnp.int32)
    start = table(CENTRE + dim).astype(jnp.int32) - span - first
    cells = lax.broadcasted_iota(jnp.int32, (count, radius.shape[1]), 0)
    step = cells - start
    if period is not None:
        step = step & (period - 1)
        inside = step <= 2 * span
    else:
        inside = (step >= 0) & (step <= 2 * span)
    spread = step.astype(jnp.float32) - (radius + table(SHIFT + dim))
    return jnp.where(inside, jnp.exp((-table(EXPONENT)) * spread * spread), 0.0)


def row_window(first, count, table, level):
    charge = jnp.where(table(LEVEL) == float(level), table(CHARGE), 0.0)
    return charge * window(first, count, table, 0, None)


def fill_depth(depth, read, slots, period):
    lanes = math.gcd(slots, 256)
    piece = math.gcd(period, 32)
    for lane in range(0, slots, lanes):
        table = read(lane, lanes)

        def body(at, carry, table=table, lane=lane):
            first = pl.multiple_of(at * piece, piece)
            depth[pl.ds(first, piece), lane : lane + lanes] = window(
                first, piece, table, 2, period
            ).astype(jnp.bfloat16)
            return carry

        lax.fori_loop(0, period // piece, body, 0, unroll=2)


def product(lhs, depth):
    return lax.dot_general(
        lhs, depth, (((1,), (1,)), ((), ())), preferred_element_type=jnp.float32
    )


def fine_kernel(level, row_tile, col_tile, period, slots):
    steps = row_tile // HALF

    def kernel(place, below, here, above, out, depth, near, cols, lhs, side):
        at = pl.program_id(0)
        first_row = place[0] * row_tile
        first_col = place[1] * col_tile

        def reader(ref, block):
            def read(lane, lanes):
                return lambda row: ref[block, row : row + 1, lane : lane + lanes]

            return read

        def whole(ref, block):
            return lambda row: ref[block, row : row + 1, :]

        def plane(row_values, rows, col_ref, col_count):
            for r in range(rows):
                for c in range(0, col_count, 16):
                    lhs[r * col_count + c : r * col_count + c + 16, :] = (
                        row_values[r : r + 1, :] * col_ref[c : c + 16, :]
                    ).astype(jnp.bfloat16)
            return lhs[0 : rows * col_count, :]

        def narrow(row_values, rows, col_values):
            for r in range(0, rows, 2):
                lhs[r * SIDE : (r + 2) * SIDE, :] = jnp.concatenate(
                    [row_values[r : r + 1, :] * col_values, row_values[r + 1 : r + 2, :] * col_values],
                    0,
                ).astype(jnp.bfloat16)
            return lhs[0 : rows * SIDE, :]

        def fill_cols(ref, block):
            def body(j, carry):
                first = pl.multiple_of(j * 16, 16)
                cols[pl.ds(first, 16), :] = window(
                    first_col + first, 16, whole(ref, block), 1, period
                )
                return carry

            lax.fori_loop(0, col_tile // 16, body, 0)

        @pl.when(at == 0)
        def _():
            for k, (block, col) in enumerate(((0, 0), (2, col_tile - SIDE))):
                for ref, row, rows in (
                    (here, 0, row_tile),
                    (below, 0, HALF),
                    (above, row_tile - HALF, HALF),
                ):
                    fill_depth(near, reader(ref, block), slots, period)
                    table = whole(ref, block)
                    col_values = window(first_col + col, SIDE, table, 1, period)
                    row_values = row_window(first_row + row, max(rows, 8), table, level)
                    part = product(narrow(row_values, rows, col_values), near[...])
                    part = part.reshape(rows, SIDE, period)
                    if ref is here:
                        side[k] = part
                    else:
                        side[k, row : row + rows] += part
            fill_depth(depth, reader(here, 1), slots, period)

        def edge(ref, row):
            fill_depth(near, reader(ref, 1), slots, period)
            fill_cols(ref, 1)
            row_values = row_window(first_row + row, 8, whole(ref, 1), level)
            part = product(plane(row_values, HALF, cols, col_tile), near[...])
            out[...] += part.reshape(HALF, col_tile, period)

        def own():
            row_values = row_window(first_row + at * HALF, 8, whole(here, 1), level)
            part = product(plane(row_values, HALF, cols, col_tile), depth[...])
            out[...] = part.reshape(HALF, col_tile, period)
            rows = pl.ds(at * HALF, HALF)
            out[:, 0:SIDE, :] += side[0, rows]
            out[:, col_tile - SIDE : col_tile, :] += side[1, rows]

        @pl.when(at == 0)
        def _():
            fill_cols(here, 1)

        own()

        @pl.when(at == 0)
        def _():
            edge(below, 0)
            fill_cols(here, 1)

        @pl.when(at == steps - 1)
        def _():
            edge(above, row_tile - HALF)

    return kernel


def fine_level(level, place, below, here, above):
    row_tile = (ROWS >> level) // lax.axis_size("brick")
    period = GRID >> level
    col_tile = period // lax.axis_size(COLUMNS)
    slots = here.shape[2]
    table_spec = pl.BlockSpec(here.shape, lambda i: (0, 0, 0))
    return pl.pallas_call(
        fine_kernel(level, row_tile, col_tile, period, slots),
        name=f"fine_{level}",
        grid=(row_tile // HALF,),
        in_specs=[pl.BlockSpec(memory_space=pltpu.SMEM), table_spec, table_spec, table_spec],
        out_specs=pl.BlockSpec((HALF, col_tile, period), lambda i: (i, 0, 0)),
        out_shape=jax.ShapeDtypeStruct((row_tile, col_tile, period), jnp.float32),
        scratch_shapes=[
            pltpu.VMEM((period, slots), jnp.bfloat16),
            pltpu.VMEM((period, slots), jnp.bfloat16),
            pltpu.VMEM((col_tile, slots), jnp.float32),
            pltpu.VMEM((max(HALF * col_tile, row_tile * SIDE), slots), jnp.bfloat16),
            pltpu.VMEM((2, row_tile, SIDE, period), jnp.float32),
        ],
        compiler_params=pltpu.CompilerParams(dimension_semantics=("arbitrary",)),
    )(place, below, here, above)


def wide_levels(place, table):
    bricks = lax.axis_size("brick")
    slots = table.shape[1]
    chunk = math.gcd(slots, 1024)
    shapes = []
    for level in range(2, 5):
        period = GRID >> level
        shapes.append((ROWS >> level, period // bricks, period))

    def kernel(place, values, *refs):
        outs, (depth, lhs) = refs[:3], refs[3:]

        @pl.when(pl.program_id(0) == 0)
        def _():
            for out in outs:
                out[...] = jnp.zeros(out.shape, jnp.float32)

        def whole(row):
            return values[row : row + 1, :]

        def read(lane, lanes):
            return lambda row: values[row : row + 1, lane : lane + lanes]

        for level, (rows, cols, period), out in zip(range(2, 5), shapes, outs):
            fill_depth(depth, read, chunk, period)
            row_values = row_window(0, rows, whole, level)
            col_values = window(place[0] * cols, max(cols, 8), whole, 1, period)
            for c in range(cols):
                lhs[c * rows : (c + 1) * rows, :] = (
                    row_values * col_values[c : c + 1, :]
                ).astype(jnp.bfloat16)
            part = product(lhs[0 : cols * rows, :], depth[0:period, :])
            for c in range(cols):
                out[:, c * period : (c + 1) * period] += part[c * rows : (c + 1) * rows, :]

    return pl.pallas_call(
        kernel,
        name="wide",
        grid=(slots // chunk,),
        in_specs=[
            pl.BlockSpec(memory_space=pltpu.SMEM),
            pl.BlockSpec((table.shape[0], chunk), lambda i: (0, i)),
        ],
        out_specs=[pl.BlockSpec((r, c * p), lambda i: (0, 0)) for r, c, p in shapes],
        out_shape=[jax.ShapeDtypeStruct((r, c * p), jnp.float32) for r, c, p in shapes],
        scratch_shapes=[
            pltpu.VMEM((GRID >> 2, chunk), jnp.bfloat16),
            pltpu.VMEM((shapes[0][0] * shapes[0][1], chunk), jnp.bfloat16),
        ],
        compiler_params=pltpu.CompilerParams(dimension_semantics=("arbitrary",)),
    )(place, table)


def per_device(
    fine_cells,
    fine_exponent,
    fine_charge,
    fine_offset,
    wide_cells,
    wide_exponent,
    wide_charge,
    wide_offset,
):
    place = jnp.stack([lax.axis_index("brick"), lax.axis_index(COLUMNS)]).astype(jnp.int32)
    mine = pack(fine_cells, fine_exponent, fine_charge, fine_offset)
    here = jnp.stack(
        [shifted(mine, COLUMNS, 1, True), mine, shifted(mine, COLUMNS, -1, True)]
    )
    below = shifted(here, "brick", 1, False)
    above = shifted(here, "brick", -1, False)
    wide = lax.all_gather(
        pack(wide_cells, wide_exponent, wide_charge, wide_offset),
        ("brick",) + COLUMNS,
        axis=1,
        tiled=True,
    )
    coarse = wide_levels(place, wide)
    first = fine_level(0, place, below, here, above)
    second = fine_level(1, place, below, here, above)
    return (first, second, coarse[0], coarse[1], coarse[2])


def solution(mesh):
    slots = ("parts", "brick", "rep", "sub")
    return jax.shard_map(
        per_device,
        mesh=mesh,
        in_specs=(
            P(None, slots),
            P(slots),
            P(slots),
            P(None, slots),
            P(None, slots),
            P(slots),
            P(slots),
            P(None, slots),
        ),
        out_specs=(
            P(("parts", "brick"), COLUMNS, None),
            P(("parts", "brick"), COLUMNS, None),
            P("parts", "brick"),
            P("parts", "brick"),
            P("parts", "brick"),
        ),
        check_vma=False,
    )
```

time: 579 us -> 80 us (0.14)
  matrix products: 330 us -> 0 us
  local copies, waits for them, and re-layouts: 99.8 us -> 1.32 us
  other arithmetic: 69.8 us -> 3.55 us
  Pallas kernels: 0 us -> 41 us
  between operations: 14.3 us -> 0.69 us
  blocking collectives: 34.2 us -> 24.4 us
  starting transfers between devices: 16.1 us -> 7.6 us
  waiting for transfers between devices: 7.63 us -> 1 us
    dot_general x46 -> x0, matrix products: 330 us -> none  [add_block(): lax.dot_general(plane_weight, depth_weight, (((0,), (0,)), ((), ())), pre...]
    dynamic_slice x91 -> x0, local copies, waits for them, and re-layouts: 61 us -> none  [the longest x44 29.8 us: add_block(): part_table = lax.dynamic_slice_in_dim(slot_table, first_slot, block_size, 1)]
    pallas_call x0 -> x3, Pallas kernels: none -> 41 us  [the longest x2 36.7 us: fine_level(): pl.pallas_call(fine_kernel(level, row_tile, col_tile, period, slots), nam...]
    select_n x91 -> x0, other arithmetic: 37.9 us -> none  [the longest x45 32.1 us: add_block(): masked = jnp.where(part_table[0] == level_index, part_charge, 0.0)]
    convert_element_type x38 -> x0, local copies, waits for them, and re-layouts: 20.1 us -> none  [add_block(): ((masked[:, None] * row_factor)[:, :, None] * col_factor[:, None, :]).ast...]
    add x90 -> x0, other arithmetic: 17.6 us -> none  [the longest x4 16.8 us: add_rims(): interior + jnp.pad(from_below, lower_widths)]
    slice x9 -> x0, local copies, waits for them, and re-layouts: 14.6 us -> none  [the longest x2 8.03 us: add_rims(): lax.slice_in_dim(tile_part, HALF, HALF + inner_count, axis=axis_dim)]
    convert_element_type x46 -> x2, other arithmetic: 9.33 us -> 1.45 us  [pack(): cells.astype(jnp.float32)]
  transfers between devices with their start and end apart: 9 -> 4, of which waited for: 2 -> 2; matrix products, arithmetic and copies ran while one was open for 12% -> 3% of each run, Pallas kernels for 0% -> 5%
where the time goes in v1:
time: 80 us; the launch traced here: 79.6 us
  Pallas kernels  41 us (51%)
  blocking collectives  24.4 us (30%)
  starting transfers between devices  7.6 us (10%)
  other arithmetic  3.55 us (4%)
  local copies, waits for them, and re-layouts  1.32 us (2%)
  waiting for transfers between devices  1 us (1%)
    pallas_call x2, Pallas kernels, fine_level(): pl.pallas_call(fine_kernel(level, row_tile, col_tile, period, slots), nam...  36.7 us
    all_gather x1, blocking collectives, per_device(): lax.all_gather(pack(wide_cells, wide_exponent, wide_charge, wide_offset),...  24.4 us
    ppermute x4, starting transfers between devices, shifted(): return lax.ppermute(array, axis, pairs)  7.6 us
    pallas_call x1, Pallas kernels, wide_levels(): pl.pallas_call(kernel, name='wide', grid=(slots // chunk,), in_specs=[pl....  4.31 us
  transfers between devices with their start and end apart: 4, of which 2 were waited for; matrix products, arithmetic and copies ran while one was open for 3% of the time, Pallas kernels for 5%

profile of v1, /device:TPU:0, one launch (start us, length us, event | category | flops | bytes accessed | tf_op | source)
XLA Modules:
  0.0 79.6 jit_solution(3685283631684907487)
XLA Ops:
  0.6 0.8 convert_element_type.6
  1.4 0.8 fusion
  2.2 0.5 collective-permute-start
  2.7 2.0 %collective-permute-start.1 = (f32[10,1024]{1,0:T(8,128)S(1)}, f32[10,1024]{1,0:T(8,128)S(1)}, u32[]{:S(2)}, u32[]{:S(2)}) collective-permute-start(f32[10,1024]{1,0:T(8,128)S(1)} %get-tuple-element.12), channel_id=1, source_target_pairs={{0,3},{1,0},{2,1},{3,2},{4,7},{5,4},{6,5},{7,6},{8,11},{9,8},{10,9... | collective-permute-start | bytes 122888 | tf_op jit(solution)/shard_map/ppermute | solution.py:27
  4.7 0.7 convert_element_type.7
  5.4 0.7 pad_maximum_fusion.2
  6.1 0.5 collective-permute-done
  6.6 0.5 collective-permute-done.1
  7.1 0.0 copy-start
  7.1 3.8 %collective-permute-start.2 = (f32[3,10,1024]{2,1,0:T(8,128)S(1)}, f32[3,10,1024]{2,1,0:T(8,128)S(1)}, u32[]{:S(2)}, u32[]{:S(2)}) collective-permute-start(f32[3,10,1024]{2,1,0:T(8,128)S(1)} %pad_maximum_fusion.here), channel_id=1, source_target_pairs={{0,4},{4,8},{8,12},{1,5},{5,9},{9,13},{2,6},{6,10},{10,14},{3,7},{... | collective-permute-start | bytes 368648 | tf_op jit(solution)/shard_map/ppermute | solution.py:27
  10.9 1.3 %collective-permute-start.3 = (f32[3,10,1024]{2,1,0:T(8,128)S(1)}, f32[3,10,1024]{2,1,0:T(8,128)S(1)}, u32[]{:S(2)}, u32[]{:S(2)}) collective-permute-start(f32[3,10,1024]{2,1,0:T(8,128)S(1)} %pad_maximum_fusion.here), channel_id=1, source_target_pairs={{4,0},{8,4},{12,8},{5,1},{9,5},{13,9},{6,2},{10,6},{14,10},{7,3},{... | collective-permute-start | bytes 368648 | tf_op jit(solution)/shard_map/ppermute | solution.py:27
  12.2 24.4 %all_gather.3.values = f32[10,2048]{1,0:T(8,128)} all-gather(f32[10,128]{1,0:T(8,128)S(1)} %pad_maximum_fusion.2), channel_id=1, replica_groups=mesh['parts'=2,'brick'=4,'rep'=2,'sub'=2] {'brick','rep','sub'}, dimensions={1}, use_global_device_ids=true | all-gather | bytes 87040 | tf_op jit(solution)/shard_map/all_gather | solution.py:262
  36.7 0.6 pad_add_fusion.place
  37.2 4.3 %wide.1 = (f32[32,4096]{1,0:T(8,128)}, f32[16,1024]{1,0:T(8,128)}, f32[8,256]{1,0:T(8,128)}) custom-call(s32[2]{0:T(128)} %pad_add_fusion.place, f32[10,2048]{1,0:T(8,128)} %all_gather.3.values), custom_call_target="tpu_custom_call" | custom-call | tf_op jit(solution)/shard_map/wide/pallas_call | solution.py:227
  41.6 0.0 collective-permute-done.2.below
  41.6 0.0 copy-start.1
  41.6 0.0 collective-permute-done.3.above
  41.6 0.0 copy-done
  41.6 0.6 copy-done.1
  42.2 0.0 copy-start.2
  42.2 0.7 copy-done.2
  42.9 24.3 %fine_0.1 = f32[32,128,512]{2,1,0:T(8,128)} custom-call(s32[2]{0:T(128)} %pad_add_fusion.place, f32[3,10,1024]{2,1,0:T(8,128)} %copy-done.1, f32[3,10,1024]{2,1,0:T(8,128)} %copy-done, f32[3,10,1024]{2,1,0:T(8,128)} %copy-done.2), custom_call_target="tpu_custom_call" | custom-call | tf_op jit(solution)/shard_map/fine_0/pallas_call | solution.py:174
  67.2 12.4 %fine_1.1 = f32[16,64,256]{2,1,0:T(8,128)} custom-call(s32[2]{0:T(128)} %pad_add_fusion.place, f32[3,10,1024]{2,1,0:T(8,128)} %copy-done.1, f32[3,10,1024]{2,1,0:T(8,128)} %copy-done, f32[3,10,1024]{2,1,0:T(8,128)} %copy-done.2), custom_call_target="tpu_custom_call" | custom-call | tf_op jit(solution)/shard_map/fine_1/pallas_call | solution.py:174
  (1 shorter events, 0.0 us)
Async XLA Ops:
  2.2 4.4 %collective-permute-start = (f32[10,1024]{1,0:T(8,128)S(1)}, f32[10,1024]{1,0:T(8,128)S(1)}, u32[]{:S(2)}, u32[]{:S(2)}) collective-permute-start(f32[10,1024]{1,0:T(8,128)S(1)} %get-tuple-element.12), channel_id=1, source_target_pairs={{0,1},{1,2},{2,3},{3,0},{4,5},{5,6},{6,7},{7,4},{8,9},{9,10},{10,1... | collective-permute-start | bytes 122888 | tf_op jit(solution)/shard_map/ppermute | solution.py:27
  2.7 4.4 %collective-permute-start.1 = (f32[10,1024]{1,0:T(8,128)S(1)}, f32[10,1024]{1,0:T(8,128)S(1)}, u32[]{:S(2)}, u32[]{:S(2)}) collective-permute-start(f32[10,1024]{1,0:T(8,128)S(1)} %get-tuple-element.12), channel_id=1, source_target_pairs={{0,3},{1,0},{2,1},{3,2},{4,7},{5,4},{6,5},{7,6},{8,11},{9,8},{10,9... | collective-permute-start | bytes 122888 | tf_op jit(solution)/shard_map/ppermute | solution.py:27
  7.1 34.5 %copy-start = (f32[3,10,1024]{2,1,0:T(8,128)}, f32[3,10,1024]{2,1,0:T(8,128)S(1)}, u32[]{:S(2)}) copy-start(f32[3,10,1024]{2,1,0:T(8,128)S(1)} %pad_maximum_fusion.here) | copy-start | bytes 368644
  7.1 34.4 %collective-permute-start.2 = (f32[3,10,1024]{2,1,0:T(8,128)S(1)}, f32[3,10,1024]{2,1,0:T(8,128)S(1)}, u32[]{:S(2)}, u32[]{:S(2)}) collective-permute-start(f32[3,10,1024]{2,1,0:T(8,128)S(1)} %pad_maximum_fusion.here), channel_id=1, source_target_pairs={{0,4},{4,8},{8,12},{1,5},{5,9},{9,13},{2,6},{6,10},{10,14},{3,7},{... | collective-permute-start | bytes 368648 | tf_op jit(solution)/shard_map/ppermute | solution.py:27
  10.9 30.7 %collective-permute-start.3 = (f32[3,10,1024]{2,1,0:T(8,128)S(1)}, f32[3,10,1024]{2,1,0:T(8,128)S(1)}, u32[]{:S(2)}, u32[]{:S(2)}) collective-permute-start(f32[3,10,1024]{2,1,0:T(8,128)S(1)} %pad_maximum_fusion.here), channel_id=1, source_target_pairs={{4,0},{8,4},{12,8},{5,1},{9,5},{13,9},{6,2},{10,6},{14,10},{7,3},{... | collective-permute-start | bytes 368648 | tf_op jit(solution)/shard_map/ppermute | solution.py:27
  41.6 0.7 copy-start.1
  42.2 0.7 copy-start.2

commit v2 on v1

v2 whole, which is shorter than its diff:
```python
import math

import jax
import jax.numpy as jnp
from jax import lax
from jax.experimental import pallas as pl
from jax.experimental.pallas import tpu as pltpu
from jax.sharding import PartitionSpec as P

GRID = 512
ROWS = 128
HALF = 4
SIDE = 8
COLUMNS = ("rep", "sub")
LEVEL, RADIUS, CENTRE, SHIFT, EXPONENT, CHARGE = 0, 1, 2, 5, 8, 9


def pack(cells, exponent, charge, offset):
    return jnp.concatenate(
        [cells.astype(jnp.float32), offset, exponent[None, :], charge[None, :]], 0
    )


def shifted(array, axis, by, wrap):
    devices = lax.axis_size(axis)
    pairs = [(i, (i + by) % devices) for i in range(devices) if wrap or 0 <= i + by < devices]
    return lax.ppermute(array, axis, pairs)


def gathered(array, axis):
    devices, width, have = lax.axis_size(axis), array.shape[1], 1
    while have < devices:
        take = min(have, devices - have)
        array = jnp.concatenate([array, shifted(array[:, : take * width], axis, have, True)], 1)
        have += take
    return array


def window(first, count, table, dim, period):
    radius = table(RADIUS)
    span = radius.astype(jnp.int32)
    start = table(CENTRE + dim).astype(jnp.int32) - span - first
    cells = lax.broadcasted_iota(jnp.int32, (count, radius.shape[1]), 0)
    step = cells - start
    if period is not None:
        step = step & (period - 1)
        inside = step <= 2 * span
    else:
        inside = (step >= 0) & (step <= 2 * span)
    spread = step.astype(jnp.float32) - (radius + table(SHIFT + dim))
    return jnp.where(inside, jnp.exp((-table(EXPONENT)) * spread * spread), 0.0)


def row_window(first, count, table, level):
    charge = jnp.where(table(LEVEL) == float(level), table(CHARGE), 0.0)
    return charge * window(first, count, table, 0, None)


def fill_depth(depth, read, slots, cells):
    lanes = math.gcd(slots, 256)
    piece = math.gcd(cells, 32)
    tall = (8, lanes)
    for lane in range(0, slots, lanes):
        table = read(lane, lanes)
        radius = table(RADIUS)
        span = radius.astype(jnp.int32)
        start = table(CENTRE + 2).astype(jnp.int32) - span
        base = lax.broadcasted_iota(jnp.int32, tall, 0) - start
        mask = jnp.broadcast_to(jnp.right_shift(GRID, table(LEVEL).astype(jnp.int32)) - 1, tall)
        width = jnp.broadcast_to(2 * span, tall)
        centre = jnp.broadcast_to(radius + table(SHIFT + 2), tall)
        decay = jnp.broadcast_to(-table(EXPONENT), tall)

        def body(at, carry, lane=lane, base=base, mask=mask, width=width, centre=centre, decay=decay):
            first = pl.multiple_of(at * piece, piece)
            for row in range(0, piece, 16):
                halves = []
                for half in range(0, 16, 8):
                    step = (base + (first + row + half)) & mask
                    spread = step.astype(jnp.float32) - centre
                    value = jnp.exp(decay * spread * spread)
                    halves.append(jnp.where(step <= width, value, 0.0))
                depth[pl.ds(first + row, 16), lane : lane + lanes] = jnp.concatenate(
                    halves, 0
                ).astype(jnp.bfloat16)
            return carry

        lax.fori_loop(0, cells // piece, body, 0, unroll=2)


def product(lhs, depth):
    return lax.dot_general(
        lhs, depth, (((1,), (1,)), ((), ())), preferred_element_type=jnp.float32
    )


def fine_kernel(sizes, slots):
    steps = sizes[0][0] // HALF

    def kernel(place, below, here, above, out, second, depth, near, cols, near_cols, lhs, side):
        at = pl.program_id(0)

        def reader(ref, block):
            def read(lane, lanes):
                return lambda row: ref[block, row : row + 1, lane : lane + lanes]

            return read

        def whole(ref, block):
            return lambda row: ref[block, row : row + 1, :]

        def row_values(ref, block, level, row, rows):
            first = place[0] * sizes[level][0] + row
            return row_window(first, max(rows, 8), whole(ref, block), level)

        def plane(values, rows, col_ref, col_count):
            for r in range(rows):
                for c in range(0, col_count, 16):
                    lhs[r * col_count + c : r * col_count + c + 16, :] = (
                        values[r : r + 1, :] * col_ref[c : c + 16, :]
                    ).astype(jnp.bfloat16)
            return lhs[0 : rows * col_count, :]

        def narrow(values, rows, col_values):
            for r in range(0, rows, 2):
                lhs[r * SIDE : (r + 2) * SIDE, :] = jnp.concatenate(
                    [values[r : r + 1, :] * col_values, values[r + 1 : r + 2, :] * col_values], 0
                ).astype(jnp.bfloat16)
            return lhs[0 : rows * SIDE, :]

        def fill_cols(target, ref, level):
            _, col_tile, period = sizes[level]

            def body(j, carry):
                first = pl.multiple_of(j * 16, 16)
                target[pl.ds(first, 16), :] = window(
                    place[1] * col_tile + first, 16, whole(ref, 1), 1, period
                )
                return carry

            lax.fori_loop(0, col_tile // 16, body, 0)

        def middle(ref, level, row, rows, col_ref, depth_ref):
            _, col_tile, period = sizes[level]
            values = row_values(ref, 1, level, row, rows)
            part = product(plane(values, rows, col_ref, col_tile), depth_ref[0:period, :])
            return part.reshape(rows, col_tile, period)

        def rim(ref, block, level, row, rows, col):
            _, col_tile, period = sizes[level]
            col_values = window(place[1] * col_tile + col, SIDE, whole(ref, block), 1, period)
            values = row_values(ref, block, level, row, rows)
            part = product(narrow(values, rows, col_values), near[0:period, :])
            return part.reshape(rows, SIDE, period)

        @pl.when(at == 0)
        def _():
            fill_depth(depth, reader(here, 1), slots, GRID)
            fill_cols(near_cols, here, 1)
            fill_cols(cols, here, 0)
            second[...] = middle(here, 1, 0, sizes[1][0], near_cols, depth)
            for k, block in enumerate((0, 2)):
                for ref in (here, below, above):
                    fill_depth(near, reader(ref, block), slots, GRID)
                    for level in (0, 1):
                        row_tile, col_tile, _ = sizes[level]
                        col = 0 if k == 0 else col_tile - SIDE
                        rows = row_tile if ref is here else HALF
                        row = row_tile - HALF if ref is above else 0
                        part = rim(ref, block, level, row, rows, col)
                        if level == 1:
                            second[row : row + rows, col : col + SIDE, :] += part
                        elif ref is here:
                            side[k] = part
                        else:
                            side[k, row : row + rows] += part

        part = middle(here, 0, at * HALF, HALF, cols, depth)
        out[...] = part
        col_tile = sizes[0][1]
        rows = pl.ds(at * HALF, HALF)
        out[:, 0:SIDE, :] += side[0, rows]
        out[:, col_tile - SIDE : col_tile, :] += side[1, rows]

        def edge(ref, top):
            fill_depth(near, reader(ref, 1), slots, GRID)
            for level in (0, 1):
                row = sizes[level][0] - HALF if top else 0
                fill_cols(near_cols, ref, level)
                part = middle(ref, level, row, HALF, near_cols, near)
                if level == 0:
                    out[...] += part
                else:
                    second[row : row + HALF] += part

        @pl.when(at == 0)
        def _():
            edge(below, False)

        @pl.when(at == steps - 1)
        def _():
            edge(above, True)

    return kernel


def fine_levels(place, below, here, above):
    sizes = []
    for level in range(2):
        period = GRID >> level
        sizes.append(
            (
                (ROWS >> level) // lax.axis_size("brick"),
                period // lax.axis_size(COLUMNS),
                period,
            )
        )
    slots = here.shape[2]
    planes = max(HALF * sizes[0][1], sizes[0][0] * SIDE, sizes[1][0] * sizes[1][1])
    table_spec = pl.BlockSpec(here.shape, lambda i: (0, 0, 0))
    return pl.pallas_call(
        fine_kernel(sizes, slots),
        name="fine",
        grid=(sizes[0][0] // HALF,),
        in_specs=[pl.BlockSpec(memory_space=pltpu.SMEM), table_spec, table_spec, table_spec],
        out_specs=[
            pl.BlockSpec((HALF,) + sizes[0][1:], lambda i: (i, 0, 0)),
            pl.BlockSpec(sizes[1], lambda i: (0, 0, 0)),
        ],
        out_shape=[jax.ShapeDtypeStruct(size, jnp.float32) for size in sizes],
        scratch_shapes=[
            pltpu.VMEM((GRID, slots), jnp.bfloat16),
            pltpu.VMEM((GRID, slots), jnp.bfloat16),
            pltpu.VMEM((sizes[0][1], slots), jnp.float32),
            pltpu.VMEM((sizes[0][1], slots), jnp.float32),
            pltpu.VMEM((planes, slots), jnp.bfloat16),
            pltpu.VMEM((2, sizes[0][0], SIDE, GRID), jnp.float32),
        ],
        compiler_params=pltpu.CompilerParams(dimension_semantics=("arbitrary",)),
    )(place, below, here, above)


def wide_levels(place, table):
    bricks = lax.axis_size("brick")
    slots = table.shape[1]
    chunk = math.gcd(slots, 1024)
    shapes = []
    for level in range(2, 5):
        period = GRID >> level
        shapes.append((ROWS >> level, period // bricks, period))

    def kernel(place, values, *refs):
        outs, (depth, lhs) = refs[:3], refs[3:]

        @pl.when(pl.program_id(0) == 0)
        def _():
            for out in outs:
                out[...] = jnp.zeros(out.shape, jnp.float32)

        def whole(row):
            return values[row : row + 1, :]

        def read(lane, lanes):
            return lambda row: values[row : row + 1, lane : lane + lanes]

        fill_depth(depth, read, chunk, GRID >> 2)
        for level, (rows, cols, period), out in zip(range(2, 5), shapes, outs):
            row_values = row_window(0, rows, whole, level)
            col_values = window(place[0] * cols, max(cols, 8), whole, 1, period)
            for c in range(cols):
                lhs[c * rows : (c + 1) * rows, :] = (
                    row_values * col_values[c : c + 1, :]
                ).astype(jnp.bfloat16)
            part = product(lhs[0 : cols * rows, :], depth[0:period, :])
            for c in range(cols):
                out[:, c * period : (c + 1) * period] += part[c * rows : (c + 1) * rows, :]

    return pl.pallas_call(
        kernel,
        name="wide",
        grid=(slots // chunk,),
        in_specs=[
            pl.BlockSpec(memory_space=pltpu.SMEM),
            pl.BlockSpec((table.shape[0], chunk), lambda i: (0, i)),
        ],
        out_specs=[pl.BlockSpec((r, c * p), lambda i: (0, 0)) for r, c, p in shapes],
        out_shape=[jax.ShapeDtypeStruct((r, c * p), jnp.float32) for r, c, p in shapes],
        scratch_shapes=[
            pltpu.VMEM((GRID >> 2, chunk), jnp.bfloat16),
            pltpu.VMEM((shapes[0][0] * shapes[0][1], chunk), jnp.bfloat16),
        ],
        compiler_params=pltpu.CompilerParams(dimension_semantics=("arbitrary",)),
    )(place, table)


def per_device(
    fine_cells,
    fine_exponent,
    fine_charge,
    fine_offset,
    wide_cells,
    wide_exponent,
    wide_charge,
    wide_offset,
):
    place = jnp.stack([lax.axis_index("brick"), lax.axis_index(COLUMNS)]).astype(jnp.int32)
    mine = pack(fine_cells, fine_exponent, fine_charge, fine_offset)
    here = jnp.stack(
        [shifted(mine, COLUMNS, 1, True), mine, shifted(mine, COLUMNS, -1, True)]
    )
    below = shifted(here, "brick", 1, False)
    above = shifted(here, "brick", -1, False)
    wide = pack(wide_cells, wide_exponent, wide_charge, wide_offset)
    wide = gathered(gathered(wide, COLUMNS), "brick")
    coarse = wide_levels(place, wide)
    first, second = fine_levels(place, below, here, above)
    return (first, second, coarse[0], coarse[1], coarse[2])


def solution(mesh):
    slots = ("parts", "brick", "rep", "sub")
    return jax.shard_map(
        per_device,
        mesh=mesh,
        in_specs=(
            P(None, slots),
            P(slots),
            P(slots),
            P(None, slots),
            P(None, slots),
            P(slots),
            P(slots),
            P(None, slots),
        ),
        out_specs=(
            P(("parts", "brick"), COLUMNS, None),
            P(("parts", "brick"), COLUMNS, None),
            P("parts", "brick"),
            P("parts", "brick"),
            P("parts", "brick"),
        ),
        check_vma=False,
    )
```

time: 80 us -> 62.1 us (0.78)
  blocking collectives: 24.4 us -> 0 us
  waiting for transfers between devices: 1 us -> 9.98 us
  Pallas kernels: 41 us -> 32.3 us
  starting transfers between devices: 7.6 us -> 11.6 us
  other arithmetic: 3.55 us -> 5.73 us
    all_gather x1 -> x0, blocking collectives: 24.4 us -> none  [per_device(): lax.all_gather(pack(wide_cells, wide_exponent, wide_charge, wide_offset),...]
    ppermute x4 -> x8, waiting for transfers between devices: 1 us -> 9.98 us  [shifted(): return lax.ppermute(array, axis, pairs)]
    pallas_call x2 -> x1, Pallas kernels: 36.7 us -> 28.1 us  [fine_levels(): pl.pallas_call(fine_kernel(sizes, slots), name='fine', grid=(sizes[0][0]...]
    ppermute x4 -> x8, starting transfers between devices: 7.6 us -> 11.6 us  [shifted(): return lax.ppermute(array, axis, pairs)]
    concatenate x0 -> x3, other arithmetic: none -> 2.17 us  [gathered(): jnp.concatenate([array, shifted(array[:, :take * width], axis, have, True...]
  transfers between devices with their start and end apart: 4 -> 8, of which waited for: 2 -> 4; matrix products, arithmetic and copies ran while one was open for 3% -> 7% of each run, Pallas kernels for 5% -> 7%
where the time goes in v2:
time: 62.1 us; the launch traced here: 61.6 us
  Pallas kernels  32.3 us (52%)
  starting transfers between devices  11.6 us (19%)
  waiting for transfers between devices  9.98 us (16%)
  other arithmetic  5.73 us (9%)
  local copies, waits for them, and re-layouts  1.34 us (2%)
  between operations  0.71 us (1%)
    pallas_call x1, Pallas kernels, fine_levels(): pl.pallas_call(fine_kernel(sizes, slots), name='fine', grid=(sizes[0][0]...  28.1 us
    ppermute x8, starting transfers between devices, shifted(): return lax.ppermute(array, axis, pairs)  11.6 us
    ppermute x8, waiting for transfers between devices, shifted(): return lax.ppermute(array, axis, pairs)  9.98 us
    pallas_call x1, Pallas kernels, wide_levels(): pl.pallas_call(kernel, name='wide', grid=(slots // chunk,), in_specs=[pl....  4.12 us
    concatenate x3, other arithmetic, gathered(): jnp.concatenate([array, shifted(array[:, :take * width], axis, have, True...  2.17 us
    convert_element_type x2, other arithmetic, pack(): cells.astype(jnp.float32)  1.45 us
    unnamed x11, local copies, waits for them, and re-layouts  1.34 us
  transfers between devices with their start and end apart: 8, of which 4 were waited for; matrix products, arithmetic and copies ran while one was open for 7% of the time, Pallas kernels for 7%

profile of v2, /device:TPU:0, one launch (start us, length us, event | category | flops | bytes accessed | tf_op | source)
XLA Modules:
  0.0 61.6 jit_solution(17376583549876703691)
XLA Ops:
  0.6 0.8 %convert_element_type.6 = f32[5,1024]{1,0:T(8,128)S(1)} convert(s32[5,1024]{1,0:T(8,128)} %param.8) | non-fusion elementwise | flops 5120 | bytes 40960 | tf_op jit(solution)/shard_map/convert_element_type | solution.py:20
  1.4 0.8 %fusion = (f32[1,10,1024]{2,1,0:T(8,128)S(1)}, f32[10,1024]{1,0:T(8,128)S(1)}) fusion(f32[1,1024]{1,0:T(1,128)} %bitcast.20, f32[1,1024]{1,0:T(1,128)} %bitcast.21, f32[3,1024]{1,0:T(4,128)} %param.11, f32[5,1024]{1,0:T(8,128)S(1)} %convert_element_type.6), kind=kLoop, calls=%fused_computation.12 | loop fusion | flops 30720 | bytes 122880 | tf_op jit(solution)/shard_map/stack | solution.py:308
  2.2 2.5 %collective-permute-start.1 = (f32[10,1024]{1,0:T(8,128)S(1)}, f32[10,1024]{1,0:T(8,128)S(1)}, u32[]{:S(2)}, u32[]{:S(2)}) collective-permute-start(f32[10,1024]{1,0:T(8,128)S(1)} %get-tuple-element.16), channel_id=1, source_target_pairs={{0,3},{1,0},{2,1},{3,2},{4,7},{5,4},{6,5},{7,6},{8,11},{9,8},{10,9... | collective-permute-start | bytes 122888 | tf_op jit(solution)/shard_map/ppermute | solution.py:27
  4.6 0.0 collective-permute-start
  4.6 0.7 %convert_element_type.7 = f32[5,128]{1,0:T(8,128)S(1)} convert(s32[5,128]{1,0:T(8,128)} %param.12) | non-fusion elementwise | flops 640 | bytes 5120 | tf_op jit(solution)/shard_map/convert_element_type | solution.py:20
  5.3 0.7 %pad_maximum_fusion.5 = (f32[10,128]{1,0:T(8,128)S(1)}, f32[10,2048]{1,0:T(8,128)S(1)}) fusion(f32[1,128]{1,0:T(1,128)} %bitcast.12, f32[1,128]{1,0:T(1,128)} %bitcast.16, f32[3,128]{1,0:T(4,128)} %param.15, f32[5,128]{1,0:T(8,128)S(1)} %convert_element_type.7), kind=kLoop, calls=%fused_computation.10 | loop fusion | flops 3839 | bytes 21504 | tf_op jit(solution)/shard_map/concatenate | solution.py:19
  6.0 0.7 %collective-permute-start.4 = (f32[10,128]{1,0:T(8,128)S(1)}, f32[10,128]{1,0:T(8,128)S(1)}, u32[]{:S(2)}, u32[]{:S(2)}) collective-permute-start(f32[10,128]{1,0:T(8,128)S(1)} %get-tuple-element.17), channel_id=1, source_target_pairs={{0,1},{1,2},{2,3},{3,0},{4,5},{5,6},{6,7},{7,4},{8,9},{9,10},{10,1... | collective-permute-start | bytes 15368 | tf_op jit(solution)/shard_map/ppermute | solution.py:27
  6.8 0.6 pad_add_fusion.place
  7.4 1.7 %collective-permute-done.4 = f32[10,128]{1,0:T(8,128)S(1)} collective-permute-done((f32[10,128]{1,0:T(8,128)S(1)}, f32[10,128]{1,0:T(8,128)S(1)}, u32[]{:S(2)}, u32[]{:S(2)}) %collective-permute-start.4) | collective-permute-done | bytes 5152 | tf_op jit(solution)/shard_map/ppermute | solution.py:27
  9.1 0.7 %pad_maximum_fusion.4 = f32[10,256]{1,0:T(8,128)S(1)} fusion(f32[10,128]{1,0:T(8,128)S(1)} %collective-permute-done.4, f32[1,128]{1,0:T(1,128)} %bitcast.13, f32[1,128]{1,0:T(1,128)} %bitcast.17, f32[3,128]{1,0:T(4,128)} %param.15, f32[5,128]{1,0:T(8,128)S(1)} %convert_element_type.7), kind=kLoop, calls=%fused_computation.4 | loop fusion | flops 10240 | bytes 20480 | tf_op jit(solution)/shard_map/concatenate | solution.py:34
  9.8 1.1 %collective-permute-start.5 = (f32[10,256]{1,0:T(8,128)S(1)}, f32[10,256]{1,0:T(8,128)S(1)}, u32[]{:S(2)}, u32[]{:S(2)}) collective-permute-start(f32[10,256]{1,0:T(8,128)S(1)} %pad_maximum_fusion.4), channel_id=1, source_target_pairs={{0,2},{1,3},{2,0},{3,1},{4,6},{5,7},{6,4},{7,5},{8,10},{9,11},{10,... | collective-permute-start | bytes 30728 | tf_op jit(solution)/shard_map/ppermute | solution.py:27
  10.9 2.7 %collective-permute-done.5 = f32[10,256]{1,0:T(8,128)S(1)} collective-permute-done((f32[10,256]{1,0:T(8,128)S(1)}, f32[10,256]{1,0:T(8,128)S(1)}, u32[]{:S(2)}, u32[]{:S(2)}) %collective-permute-start.5) | collective-permute-done | bytes 10272 | tf_op jit(solution)/shard_map/ppermute | solution.py:27
  13.6 0.7 %pad_maximum_fusion.3 = f32[10,512]{1,0:T(8,128)S(1)} fusion(f32[10,256]{1,0:T(8,128)S(1)} %collective-permute-done.5, f32[10,128]{1,0:T(8,128)S(1)} %collective-permute-done.4, f32[1,128]{1,0:T(1,128)} %bitcast.14, f32[1,128]{1,0:T(1,128)} %bitcast.18, f32[3,128]{1,0:T(4,128)} %param.15, f32[5,128]{1,0:T(8,128)S(1)} %convert_element_type.7), kind=kLoop, calls=%fused_computation.3 | loop fusion | flops 25600 | bytes 40960 | tf_op jit(solution)/shard_map/concatenate | solution.py:34
  14.3 1.6 %collective-permute-start.6 = (f32[10,512]{1,0:T(8,128)S(1)}, f32[10,512]{1,0:T(8,128)S(1)}, u32[]{:S(2)}, u32[]{:S(2)}) collective-permute-start(f32[10,512]{1,0:T(8,128)S(1)} %pad_maximum_fusion.3), channel_id=1, source_target_pairs={{0,4},{4,8},{8,12},{12,0},{1,5},{5,9},{9,13},{13,1},{2,6},{6,10},{... | collective-permute-start | bytes 61448 | tf_op jit(solution)/shard_map/ppermute | solution.py:27
  16.0 4.1 %collective-permute-done.6 = f32[10,512]{1,0:T(8,128)S(1)} collective-permute-done((f32[10,512]{1,0:T(8,128)S(1)}, f32[10,512]{1,0:T(8,128)S(1)}, u32[]{:S(2)}, u32[]{:S(2)}) %collective-permute-start.6) | collective-permute-done | bytes 20512 | tf_op jit(solution)/shard_map/ppermute | solution.py:27
  20.1 0.7 %pad_maximum_fusion.2 = f32[10,1024]{1,0:T(8,128)S(1)} fusion(f32[10,512]{1,0:T(8,128)S(1)} %collective-permute-done.6, f32[10,256]{1,0:T(8,128)S(1)} %collective-permute-done.5, f32[10,128]{1,0:T(8,128)S(1)} %collective-permute-done.4, f32[1,128]{1,0:T(1,128)} %bitcast.15, f32[1,128]{1,0:T(1,128)} %bitcast.19, f32[3,128]{1,0:T(4,128)} %param.15, ...), kind=kLoop, calls=%fused_computation.2 | loop fusion | flops 61440 | bytes 81920 | tf_op jit(solution)/shard_map/concatenate | solution.py:34
  20.8 0.9 %collective-permute-start.7 = (f32[10,1024]{1,0:T(8,128)S(1)}, f32[10,1024]{1,0:T(8,128)S(1)}, u32[]{:S(2)}, u32[]{:S(2)}) collective-permute-start(f32[10,1024]{1,0:T(8,128)S(1)} %pad_maximum_fusion.2), channel_id=1, source_target_pairs={{0,8},{4,12},{8,0},{12,4},{1,9},{5,13},{9,1},{13,5},{2,10},{6,14},... | collective-permute-start | bytes 122888 | tf_op jit(solution)/shard_map/ppermute | solution.py:27
  21.7 0.0 collective-permute-done.1
  21.7 0.0 collective-permute-done
  21.7 0.0 copy-start
  21.7 3.5 %collective-permute-start.2 = (f32[3,10,1024]{2,1,0:T(8,128)S(1)}, f32[3,10,1024]{2,1,0:T(8,128)S(1)}, u32[]{:S(2)}, u32[]{:S(2)}) collective-permute-start(f32[3,10,1024]{2,1,0:T(8,128)S(1)} %pad_maximum_fusion.here), channel_id=1, source_target_pairs={{0,4},{4,8},{8,12},{1,5},{5,9},{9,13},{2,6},{6,10},{10,14},{3,7},{... | collective-permute-start | bytes 368648 | tf_op jit(solution)/shard_map/ppermute | solution.py:27
  25.2 1.3 %collective-permute-start.3 = (f32[3,10,1024]{2,1,0:T(8,128)S(1)}, f32[3,10,1024]{2,1,0:T(8,128)S(1)}, u32[]{:S(2)}, u32[]{:S(2)}) collective-permute-start(f32[3,10,1024]{2,1,0:T(8,128)S(1)} %pad_maximum_fusion.here), channel_id=1, source_target_pairs={{4,0},{8,4},{12,8},{5,1},{9,5},{13,9},{6,2},{10,6},{14,10},{7,3},{... | collective-permute-start | bytes 368648 | tf_op jit(solution)/shard_map/ppermute | solution.py:27
  26.5 0.0 collective-permute-done.7
  26.5 0.0 copy-start.3
  26.6 0.6 %copy-done.3 = f32[10,2048]{1,0:T(8,128)} copy-done((f32[10,2048]{1,0:T(8,128)}, f32[10,2048]{1,0:T(8,128)S(1)}, u32[]{:S(2)}) %copy-start.3) | copy-done | bytes 81944
  27.2 4.1 %wide.1 = (f32[32,4096]{1,0:T(8,128)}, f32[16,1024]{1,0:T(8,128)}, f32[8,256]{1,0:T(8,128)}) custom-call(s32[2]{0:T(128)} %pad_add_fusion.place, f32[10,2048]{1,0:T(8,128)} %copy-done.3), custom_call_target="tpu_custom_call" | custom-call | tf_op jit(solution)/shard_map/wide/pallas_call | solution.py:278
  31.3 0.0 collective-permute-done.2.below
  31.3 0.0 copy-start.1
  31.3 1.4 %collective-permute-done.3.above = f32[3,10,1024]{2,1,0:T(8,128)S(1)} collective-permute-done((f32[3,10,1024]{2,1,0:T(8,128)S(1)}, f32[3,10,1024]{2,1,0:T(8,128)S(1)}, u32[]{:S(2)}, u32[]{:S(2)}) %collective-permute-start.3) | collective-permute-done | bytes 122912 | tf_op jit(solution)/shard_map/ppermute | solution.py:27
  32.8 0.0 copy-done
  32.8 0.0 copy-done.1
  32.8 0.0 copy-start.2
  32.8 0.7 %copy-done.2 = f32[3,10,1024]{2,1,0:T(8,128)} copy-done((f32[3,10,1024]{2,1,0:T(8,128)}, f32[3,10,1024]{2,1,0:T(8,128)S(1)}, u32[]{:S(2)}) %copy-start.2) | copy-done | bytes 122904
  33.4 28.1 %fine.1 = (f32[32,128,512]{2,1,0:T(8,128)}, f32[16,64,256]{2,1,0:T(8,128)}) custom-call(s32[2]{0:T(128)} %pad_add_fusion.place, f32[3,10,1024]{2,1,0:T(8,128)} %copy-done.1, f32[3,10,1024]{2,1,0:T(8,128)} %copy-done, f32[3,10,1024]{2,1,0:T(8,128)} %copy-done.2), custom_call_target="tpu_custom_call" | custom-call | tf_op jit(solution)/shard_map/fine/pallas_call | solution.py:221
  (5 shorter events, 0.0 us)
Async XLA Ops:
  2.2 19.5 %collective-permute-start.1 = (f32[10,1024]{1,0:T(8,128)S(1)}, f32[10,1024]{1,0:T(8,128)S(1)}, u32[]{:S(2)}, u32[]{:S(2)}) collective-permute-start(f32[10,1024]{1,0:T(8,128)S(1)} %get-tuple-element.16), channel_id=1, source_target_pairs={{0,3},{1,0},{2,1},{3,2},{4,7},{5,4},{6,5},{7,6},{8,11},{9,8},{10,9... | collective-permute-start | bytes 122888 | tf_op jit(solution)/shard_map/ppermute | solution.py:27
  4.6 17.0 %collective-permute-start = (f32[10,1024]{1,0:T(8,128)S(1)}, f32[10,1024]{1,0:T(8,128)S(1)}, u32[]{:S(2)}, u32[]{:S(2)}) collective-permute-start(f32[10,1024]{1,0:T(8,128)S(1)} %get-tuple-element.16), channel_id=1, source_target_pairs={{0,1},{1,2},{2,3},{3,0},{4,5},{5,6},{6,7},{7,4},{8,9},{9,10},{10,1... | collective-permute-start | bytes 122888 | tf_op jit(solution)/shard_map/ppermute | solution.py:27
  6.0 3.1 %collective-permute-start.4 = (f32[10,128]{1,0:T(8,128)S(1)}, f32[10,128]{1,0:T(8,128)S(1)}, u32[]{:S(2)}, u32[]{:S(2)}) collective-permute-start(f32[10,128]{1,0:T(8,128)S(1)} %get-tuple-element.17), channel_id=1, source_target_pairs={{0,1},{1,2},{2,3},{3,0},{4,5},{5,6},{6,7},{7,4},{8,9},{9,10},{10,1... | collective-permute-start | bytes 15368 | tf_op jit(solution)/shard_map/ppermute | solution.py:27
  9.8 3.8 %collective-permute-start.5 = (f32[10,256]{1,0:T(8,128)S(1)}, f32[10,256]{1,0:T(8,128)S(1)}, u32[]{:S(2)}, u32[]{:S(2)}) collective-permute-start(f32[10,256]{1,0:T(8,128)S(1)} %pad_maximum_fusion.4), channel_id=1, source_target_pairs={{0,2},{1,3},{2,0},{3,1},{4,6},{5,7},{6,4},{7,5},{8,10},{9,11},{10,... | collective-permute-start | bytes 30728 | tf_op jit(solution)/shard_map/ppermute | solution.py:27
  14.3 5.7 %collective-permute-start.6 = (f32[10,512]{1,0:T(8,128)S(1)}, f32[10,512]{1,0:T(8,128)S(1)}, u32[]{:S(2)}, u32[]{:S(2)}) collective-permute-start(f32[10,512]{1,0:T(8,128)S(1)} %pad_maximum_fusion.3), channel_id=1, source_target_pairs={{0,4},{4,8},{8,12},{12,0},{1,5},{5,9},{9,13},{13,1},{2,6},{6,10},{... | collective-permute-start | bytes 61448 | tf_op jit(solution)/shard_map/ppermute | solution.py:27
  20.8 5.7 %collective-permute-start.7 = (f32[10,1024]{1,0:T(8,128)S(1)}, f32[10,1024]{1,0:T(8,128)S(1)}, u32[]{:S(2)}, u32[]{:S(2)}) collective-permute-start(f32[10,1024]{1,0:T(8,128)S(1)} %pad_maximum_fusion.2), channel_id=1, source_target_pairs={{0,8},{4,12},{8,0},{12,4},{1,9},{5,13},{9,1},{13,5},{2,10},{6,14},... | collective-permute-start | bytes 122888 | tf_op jit(solution)/shard_map/ppermute | solution.py:27
  21.7 11.1 %copy-start = (f32[3,10,1024]{2,1,0:T(8,128)}, f32[3,10,1024]{2,1,0:T(8,128)S(1)}, u32[]{:S(2)}) copy-start(f32[3,10,1024]{2,1,0:T(8,128)S(1)} %pad_maximum_fusion.here) | copy-start | bytes 368644
  21.7 9.6 %collective-permute-start.2 = (f32[3,10,1024]{2,1,0:T(8,128)S(1)}, f32[3,10,1024]{2,1,0:T(8,128)S(1)}, u32[]{:S(2)}, u32[]{:S(2)}) collective-permute-start(f32[3,10,1024]{2,1,0:T(8,128)S(1)} %pad_maximum_fusion.here), channel_id=1, source_target_pairs={{0,4},{4,8},{8,12},{1,5},{5,9},{9,13},{2,6},{6,10},{10,14},{3,7},{... | collective-permute-start | bytes 368648 | tf_op jit(solution)/shard_map/ppermute | solution.py:27
  25.2 7.6 %collective-permute-start.3 = (f32[3,10,1024]{2,1,0:T(8,128)S(1)}, f32[3,10,1024]{2,1,0:T(8,128)S(1)}, u32[]{:S(2)}, u32[]{:S(2)}) collective-permute-start(f32[3,10,1024]{2,1,0:T(8,128)S(1)} %pad_maximum_fusion.here), channel_id=1, source_target_pairs={{4,0},{8,4},{12,8},{5,1},{9,5},{13,9},{6,2},{10,6},{14,10},{7,3},{... | collective-permute-start | bytes 368648 | tf_op jit(solution)/shard_map/ppermute | solution.py:27
  26.5 0.7 %copy-start.3 = (f32[10,2048]{1,0:T(8,128)}, f32[10,2048]{1,0:T(8,128)S(1)}, u32[]{:S(2)}) copy-start(f32[10,2048]{1,0:T(8,128)S(1)} %constant_dynamic-update-slice_fusion.values) | copy-start | bytes 245764
  31.3 1.4 %copy-start.1 = (f32[3,10,1024]{2,1,0:T(8,128)}, f32[3,10,1024]{2,1,0:T(8,128)S(1)}, u32[]{:S(2)}) copy-start(f32[3,10,1024]{2,1,0:T(8,128)S(1)} %collective-permute-done.2.below) | copy-start | bytes 368644
  32.8 0.7 %copy-start.2 = (f32[3,10,1024]{2,1,0:T(8,128)}, f32[3,10,1024]{2,1,0:T(8,128)S(1)}, u32[]{:S(2)}) copy-start(f32[3,10,1024]{2,1,0:T(8,128)S(1)} %collective-permute-done.3.above) | copy-start | bytes 368644

commit v3 on v2

--- a/solution.py
+++ b/solution.py
@@ -21,19 +21,9 @@
     )
 
 
-def shifted(array, axis, by, wrap):
+def shifted(array, axis, by):
     devices = lax.axis_size(axis)
-    pairs = [(i, (i + by) % devices) for i in range(devices) if wrap or 0 <= i + by < devices]
-    return lax.ppermute(array, axis, pairs)
-
-
-def gathered(array, axis):
-    devices, width, have = lax.axis_size(axis), array.shape[1], 1
-    while have < devices:
-        take = min(have, devices - have)
-        array = jnp.concatenate([array, shifted(array[:, : take * width], axis, have, True)], 1)
-        have += take
-    return array
+    return lax.ppermute(array, axis, [(i, (i + by) % devices) for i in range(devices)])
 
 
 def window(first, count, table, dim, period):
@@ -94,7 +84,7 @@
     )
 
 
-def fine_kernel(sizes, slots):
+def fine_kernel(sizes, slots, stride):
     steps = sizes[0][0] // HALF
 
     def kernel(place, below, here, above, out, second, depth, near, cols, near_cols, lhs, side):
@@ -102,12 +92,13 @@
 
         def reader(ref, block):
             def read(lane, lanes):
-                return lambda row: ref[block, row : row + 1, lane : lane + lanes]
+                first = block * stride + lane
+                return lambda row: ref[row : row + 1, first : first + lanes]
 
             return read
 
         def whole(ref, block):
-            return lambda row: ref[block, row : row + 1, :]
+            return lambda row: ref[row : row + 1, block * stride : block * stride + slots]
 
         def row_values(ref, block, level, row, rows):
             first = place[0] * sizes[level][0] + row
@@ -204,7 +195,7 @@
     return kernel
 
 
-def fine_levels(place, below, here, above):
+def fine_levels(place, below, here, above, slots, stride):
     sizes = []
     for level in range(2):
         period = GRID >> level
@@ -215,11 +206,10 @@
                 period,
             )
         )
-    slots = here.shape[2]
     planes = max(HALF * sizes[0][1], sizes[0][0] * SIDE, sizes[1][0] * sizes[1][1])
-    table_spec = pl.BlockSpec(here.shape, lambda i: (0, 0, 0))
+    table_spec = pl.BlockSpec(here.shape, lambda i: (0, 0))
     return pl.pallas_call(
-        fine_kernel(sizes, slots),
+        fine_kernel(sizes, slots, stride),
         name="fine",
         grid=(sizes[0][0] // HALF,),
         in_specs=[pl.BlockSpec(memory_space=pltpu.SMEM), table_spec, table_spec, table_spec],
@@ -304,16 +294,33 @@
     wide_offset,
 ):
     place = jnp.stack([lax.axis_index("brick"), lax.axis_index(COLUMNS)]).astype(jnp.int32)
-    mine = pack(fine_cells, fine_exponent, fine_charge, fine_offset)
-    here = jnp.stack(
-        [shifted(mine, COLUMNS, 1, True), mine, shifted(mine, COLUMNS, -1, True)]
+    slots = fine_exponent.shape[0]
+    stride = slots + wide_exponent.shape[0]
+    mine = jnp.concatenate(
+        [
+            pack(fine_cells, fine_exponent, fine_charge, fine_offset),
+            pack(wide_cells, wide_exponent, wide_charge, wide_offset),
+        ],
+        1,
     )
-    below = shifted(here, "brick", 1, False)
-    above = shifted(here, "brick", -1, False)
-    wide = pack(wide_cells, wide_exponent, wide_charge, wide_offset)
-    wide = gathered(gathered(wide, COLUMNS), "brick")
+
+    def wides(block):
+        near = [block[:, b * stride + slots : (b + 1) * stride] for b in range(3)]
+        return near + [block[:, 3 * stride :]]
+
+    left = shifted(mine, COLUMNS, 1)
+    right = shifted(mine, COLUMNS, -1)
+    others = [
+        shifted(mine[:, slots:], COLUMNS, by) for by in range(2, lax.axis_size(COLUMNS) - 1)
+    ]
+    here = jnp.concatenate([left, mine, right] + others, 1)
+    below = shifted(here, "brick", 1)
+    above = shifted(here, "brick", -1)
+    column = jnp.concatenate(wides(here), 1)
+    far = [shifted(column, "brick", by) for by in range(2, lax.axis_size("brick") - 1)]
+    wide = jnp.concatenate([column] + wides(below) + wides(above) + far, 1)
     coarse = wide_levels(place, wide)
-    first, second = fine_levels(place, below, here, above)
+    first, second = fine_levels(place, below, here, above, slots, stride)
     return (first, second, coarse[0], coarse[1], coarse[2])
 
 

time: 62.1 us -> 61.2 us (0.986)
  waiting for transfers between devices: 9.98 us -> 11.8 us
  starting transfers between devices: 11.6 us -> 10.1 us
  local copies, waits for them, and re-layouts: 1.34 us -> 0.7 us
    ppermute x8 -> x6, waiting for transfers between devices: 9.98 us -> 11.8 us  [shifted(): lax.ppermute(array, axis, [(i, (i + by) % devices) for i in range(devices)])]
    unnamed x0 -> x2, other arithmetic: none -> 1.5 us
    ppermute x8 -> x6, starting transfers between devices: 11.6 us -> 10.1 us  [shifted(): lax.ppermute(array, axis, [(i, (i + by) % devices) for i in range(devices)])]
    concatenate x4 -> x2, other arithmetic: 2.89 us -> 1.54 us  [the longest x1 0.82 us: per_device(): jnp.concatenate([pack(fine_cells, fine_exponent, fine_charge, fine_offset...]
    another operation x2 -> x0, other arithmetic: 0.79 us -> none  [per_device(): jnp.stack([shifted(mine, COLUMNS, 1, True), mine, shifted(mine, COLUMNS,...]
    unnamed x11 -> x17, local copies, waits for them, and re-layouts: 1.34 us -> 0.69 us
  transfers between devices with their start and end apart: 8 -> 6, of which waited for: 4 -> 5; matrix products, arithmetic and copies ran while one was open for 7% -> 5% of each run, Pallas kernels for 7% -> 0%
where the time goes in v3:
time: 61.2 us; the launch traced here: 60.8 us
  Pallas kernels  32.3 us (53%)
  waiting for transfers between devices  11.8 us (19%)
  starting transfers between devices  10.1 us (17%)
  other arithmetic  5.14 us (8%)
  local copies, waits for them, and re-layouts  0.7 us (1%)
  between operations  0.69 us (1%)
    pallas_call x1, Pallas kernels, fine_levels(): pl.pallas_call(fine_kernel(sizes, slots, stride), name='fine', grid=(size...  28.2 us
    ppermute x6, waiting for transfers between devices, shifted(): lax.ppermute(array, axis, [(i, (i + by) % devices) for i in range(devices)])  11.8 us
    ppermute x6, starting transfers between devices, shifted(): lax.ppermute(array, axis, [(i, (i + by) % devices) for i in range(devices)])  10.1 us
    pallas_call x1, Pallas kernels, wide_levels(): pl.pallas_call(kernel, name='wide', grid=(slots // chunk,), in_specs=[pl....  4.11 us
    unnamed x2, other arithmetic  1.5 us
    convert_element_type x2, other arithmetic, pack(): cells.astype(jnp.float32)  1.45 us
  transfers between devices with their start and end apart: 6, of which 5 were waited for; matrix products, arithmetic and copies ran while one was open for 5% of the time, Pallas kernels for 0%

profile of v3, /device:TPU:0, one launch (start us, length us, event | category | flops | bytes accessed | tf_op | source)
XLA Modules:
  0.0 60.8 jit_solution(17821236945124772920)
XLA Ops:
  0.6 0.7 %convert_element_type.7 = f32[5,128]{1,0:T(8,128)S(1)} convert(s32[5,128]{1,0:T(8,128)} %param.12) | non-fusion elementwise | flops 640 | bytes 5120 | tf_op jit(solution)/shard_map/convert_element_type | solution.py:20
  1.3 0.8 %convert_element_type.6 = f32[5,1024]{1,0:T(8,128)S(1)} convert(s32[5,1024]{1,0:T(8,128)} %param.8) | non-fusion elementwise | flops 5120 | bytes 40960 | tf_op jit(solution)/shard_map/convert_element_type | solution.py:20
  2.1 0.8 %maximum_maximum_fusion = f32[10,1152]{1,0:T(8,128)S(1)} fusion(f32[1,128]{1,0:T(1,128)} %bitcast.10, f32[1,128]{1,0:T(1,128)} %bitcast.13, f32[3,128]{1,0:T(4,128)} %param.15, f32[5,128]{1,0:T(8,128)S(1)} %convert_element_type.7, f32[1,1024]{1,0:T(1,128)} %bitcast.6, f32[1,1024]{1,0:T(1,128)} %bitcast.8, f32[3,1024]{1,0:T(4,128)} %param.11, ...), kind=kLoop, calls=%fused_computation | loop fusion | flops 80640 | bytes 92160 | tf_op jit(solution)/shard_map/concatenate | solution.py:299
  2.9 0.5 collective-permute-start
  3.4 2.0 %collective-permute-start.1 = (f32[10,1152]{1,0:T(8,128)S(1)}, f32[10,1152]{1,0:T(8,128)S(1)}, u32[]{:S(2)}, u32[]{:S(2)}) collective-permute-start(f32[10,1152]{1,0:T(8,128)S(1)} %maximum_maximum_fusion), channel_id=1, source_target_pairs={{0,3},{1,0},{2,1},{3,2},{4,7},{5,4},{6,5},{7,6},{8,11},{9,8},{10,9... | collective-permute-start | bytes 138248 | tf_op jit(solution)/shard_map/ppermute | solution.py:26
  5.4 2.0 %collective-permute-done = f32[10,1152]{1,0:T(8,128)S(1)} collective-permute-done((f32[10,1152]{1,0:T(8,128)S(1)}, f32[10,1152]{1,0:T(8,128)S(1)}, u32[]{:S(2)}, u32[]{:S(2)}) %collective-permute-start) | collective-permute-done | bytes 46112 | tf_op jit(solution)/shard_map/ppermute | solution.py:26
  7.4 0.8 %maximum_dynamic-update-slice_fusion = f32[10,3584]{1,0:T(8,128)S(1)} fusion(f32[10,3584]{1,0:T(8,128)S(1)} %constant_dynamic-update-slice_fusion.3, f32[1,1024]{1,0:T(1,128)} %bitcast.7, f32[1,1024]{1,0:T(1,128)} %bitcast.9, f32[3,1024]{1,0:T(4,128)} %param.11, f32[5,1024]{1,0:T(8,128)S(1)} %convert_element_type.6), kind=kLoop, calls=%fused_computation.1 | loop fusion | flops 30720 | bytes 118784
  8.2 0.7 %constant_dynamic-update-slice_fusion.13 = (f32[10,2048]{1,0:T(8,128)S(1)}, f32[10,3584]{1,0:T(8,128)S(1)}, f32[10,128]{1,0:T(8,128)S(1)}) fusion(f32[10,2048]{1,0:T(8,128)S(1)} %get-tuple-element.16, f32[1,128]{1,0:T(1,128)} %bitcast.11, f32[1,128]{1,0:T(1,128)} %bitcast.14, f32[3,128]{1,0:T(4,128)} %param.15, f32[5,128]{1,0:T(8,128)S(1)} %convert_element_type.7, ...), kind=kLoop, calls=%fused_computation.15 | loop fusion | flops 3840 | bytes 31232
  8.9 3.1 %collective-permute-start.2 = (f32[10,128]{1,0:T(8,128)S(1)}, f32[10,128]{1,0:T(8,128)S(1)}, u32[]{:S(2)}, u32[]{:S(2)}) collective-permute-start(f32[10,128]{1,0:T(8,128)S(1)} %get-tuple-element.23), channel_id=1, source_target_pairs={{0,2},{1,3},{2,0},{3,1},{4,6},{5,7},{6,4},{7,5},{8,10},{9,11},{10,... | collective-permute-start | bytes 15368 | tf_op jit(solution)/shard_map/ppermute | solution.py:26
  12.0 0.0 collective-permute-done.1
  12.0 1.6 %collective-permute-done.2 = f32[10,128]{1,0:T(8,128)S(1)} collective-permute-done((f32[10,128]{1,0:T(8,128)S(1)}, f32[10,128]{1,0:T(8,128)S(1)}, u32[]{:S(2)}, u32[]{:S(2)}) %collective-permute-start.2) | collective-permute-done | bytes 5152 | tf_op jit(solution)/shard_map/ppermute | solution.py:26
  13.6 0.0 copy-start
  13.6 1.4 %collective-permute-start.3 = (f32[10,3584]{1,0:T(8,128)S(1)}, f32[10,3584]{1,0:T(8,128)S(1)}, u32[]{:S(2)}, u32[]{:S(2)}) collective-permute-start(f32[10,3584]{1,0:T(8,128)S(1)} %get-tuple-element.20.here), channel_id=1, source_target_pairs={{0,4},{4,8},{8,12},{12,0},{1,5},{5,9},{9,13},{13,1},{2,6},{6,10},{... | collective-permute-start | bytes 430088 | tf_op jit(solution)/shard_map/ppermute | solution.py:26
  15.0 0.6 %pad_add_fusion.place = s32[2]{0:T(128)} fusion(s32[1]{0:T(128)} %bitcast.1, s32[1]{0:T(128)} %bitcast), kind=kLoop, calls=%fused_computation.19 | loop fusion | flops 2 | bytes 16 | tf_op jit(solution)/shard_map/stack | solution.py:296
  15.7 2.4 %collective-permute-start.4 = (f32[10,3584]{1,0:T(8,128)S(1)}, f32[10,3584]{1,0:T(8,128)S(1)}, u32[]{:S(2)}, u32[]{:S(2)}) collective-permute-start(f32[10,3584]{1,0:T(8,128)S(1)} %get-tuple-element.20.here), channel_id=1, source_target_pairs={{0,12},{4,0},{8,4},{12,8},{1,13},{5,1},{9,5},{13,9},{2,14},{6,2},{... | collective-permute-start | bytes 430088 | tf_op jit(solution)/shard_map/ppermute | solution.py:26
  18.1 0.7 %pad_maximum_fusion = f32[10,512]{1,0:T(8,128)S(1)} fusion(f32[10,128]{1,0:T(8,128)S(1)} %collective-permute-done.2, f32[10,128]{1,0:T(8,128)S(1)} %get-tuple-element.17, f32[1,128]{1,0:T(1,128)} %bitcast.12, f32[1,128]{1,0:T(1,128)} %bitcast.15, f32[3,128]{1,0:T(4,128)} %param.15, f32[5,128]{1,0:T(8,128)S(1)} %convert_element_type.7, ...), kind=kLoop, calls=%fused_computation.17 | loop fusion | flops 30720 | bytes 40960 | tf_op jit(solution)/shard_map/concatenate | solution.py:319
  18.8 0.7 %collective-permute-start.5 = (f32[10,512]{1,0:T(8,128)S(1)}, f32[10,512]{1,0:T(8,128)S(1)}, u32[]{:S(2)}, u32[]{:S(2)}) collective-permute-start(f32[10,512]{1,0:T(8,128)S(1)} %pad_maximum_fusion), channel_id=1, source_target_pairs={{0,8},{4,12},{8,0},{12,4},{1,9},{5,13},{9,1},{13,5},{2,10},{6,14},... | collective-permute-start | bytes 61448 | tf_op jit(solution)/shard_map/ppermute | solution.py:26
  19.5 4.4 %collective-permute-done.3.below = f32[10,3584]{1,0:T(8,128)S(1)} collective-permute-done((f32[10,3584]{1,0:T(8,128)S(1)}, f32[10,3584]{1,0:T(8,128)S(1)}, u32[]{:S(2)}, u32[]{:S(2)}) %collective-permute-start.3) | collective-permute-done | bytes 143392 | tf_op jit(solution)/shard_map/ppermute | solution.py:26
  23.9 0.0 copy-start.1
  23.9 2.0 %collective-permute-done.4.above = f32[10,3584]{1,0:T(8,128)S(1)} collective-permute-done((f32[10,3584]{1,0:T(8,128)S(1)}, f32[10,3584]{1,0:T(8,128)S(1)}, u32[]{:S(2)}, u32[]{:S(2)}) %collective-permute-start.4) | collective-permute-done | bytes 143392 | tf_op jit(solution)/shard_map/ppermute | solution.py:26
  25.9 0.0 copy-start.2
  25.9 1.8 %collective-permute-done.5 = f32[10,512]{1,0:T(8,128)S(1)} collective-permute-done((f32[10,512]{1,0:T(8,128)S(1)}, f32[10,512]{1,0:T(8,128)S(1)}, u32[]{:S(2)}, u32[]{:S(2)}) %collective-permute-start.5) | collective-permute-done | bytes 20512 | tf_op jit(solution)/shard_map/ppermute | solution.py:26
  27.7 0.0 copy-start.3
  27.8 0.7 %copy-done.3 = f32[10,2048]{1,0:T(8,128)} copy-done((f32[10,2048]{1,0:T(8,128)}, f32[10,2048]{1,0:T(8,128)S(1)}, u32[]{:S(2)}) %copy-start.3) | copy-done | bytes 81944
  28.4 4.1 %wide.1 = (f32[32,4096]{1,0:T(8,128)}, f32[16,1024]{1,0:T(8,128)}, f32[8,256]{1,0:T(8,128)}) custom-call(s32[2]{0:T(128)} %pad_add_fusion.place, f32[10,2048]{1,0:T(8,128)} %copy-done.3), custom_call_target="tpu_custom_call" | custom-call | tf_op jit(solution)/shard_map/wide/pallas_call | solution.py:268
  32.5 0.0 copy-done
  32.5 0.0 copy-done.1
  32.5 0.0 copy-done.2
  32.5 28.2 %fine.1 = (f32[32,128,512]{2,1,0:T(8,128)}, f32[16,64,256]{2,1,0:T(8,128)}) custom-call(s32[2]{0:T(128)} %pad_add_fusion.place, f32[10,3584]{1,0:T(8,128)} %copy-done.1, f32[10,3584]{1,0:T(8,128)} %copy-done, f32[10,3584]{1,0:T(8,128)} %copy-done.2), custom_call_target="tpu_custom_call" | custom-call | tf_op jit(solution)/shard_map/fine/pallas_call | solution.py:211
  (12 shorter events, 0.0 us)
Async XLA Ops:
  2.9 4.5 %collective-permute-start = (f32[10,1152]{1,0:T(8,128)S(1)}, f32[10,1152]{1,0:T(8,128)S(1)}, u32[]{:S(2)}, u32[]{:S(2)}) collective-permute-start(f32[10,1152]{1,0:T(8,128)S(1)} %maximum_maximum_fusion), channel_id=1, source_target_pairs={{0,1},{1,2},{2,3},{3,0},{4,5},{5,6},{6,7},{7,4},{8,9},{9,10},{10,1... | collective-permute-start | bytes 138248 | tf_op jit(solution)/shard_map/ppermute | solution.py:26
  3.4 8.5 %collective-permute-start.1 = (f32[10,1152]{1,0:T(8,128)S(1)}, f32[10,1152]{1,0:T(8,128)S(1)}, u32[]{:S(2)}, u32[]{:S(2)}) collective-permute-start(f32[10,1152]{1,0:T(8,128)S(1)} %maximum_maximum_fusion), channel_id=1, source_target_pairs={{0,3},{1,0},{2,1},{3,2},{4,7},{5,4},{6,5},{7,6},{8,11},{9,8},{10,9... | collective-permute-start | bytes 138248 | tf_op jit(solution)/shard_map/ppermute | solution.py:26
  8.9 4.7 %collective-permute-start.2 = (f32[10,128]{1,0:T(8,128)S(1)}, f32[10,128]{1,0:T(8,128)S(1)}, u32[]{:S(2)}, u32[]{:S(2)}) collective-permute-start(f32[10,128]{1,0:T(8,128)S(1)} %get-tuple-element.23), channel_id=1, source_target_pairs={{0,2},{1,3},{2,0},{3,1},{4,6},{5,7},{6,4},{7,5},{8,10},{9,11},{10,... | collective-permute-start | bytes 15368 | tf_op jit(solution)/shard_map/ppermute | solution.py:26
  13.6 18.9 %copy-start = (f32[10,3584]{1,0:T(8,128)}, f32[10,3584]{1,0:T(8,128)S(1)}, u32[]{:S(2)}) copy-start(f32[10,3584]{1,0:T(8,128)S(1)} %get-tuple-element.20.here) | copy-start | bytes 430084
  13.6 10.3 %collective-permute-start.3 = (f32[10,3584]{1,0:T(8,128)S(1)}, f32[10,3584]{1,0:T(8,128)S(1)}, u32[]{:S(2)}, u32[]{:S(2)}) collective-permute-start(f32[10,3584]{1,0:T(8,128)S(1)} %get-tuple-element.20.here), channel_id=1, source_target_pairs={{0,4},{4,8},{8,12},{12,0},{1,5},{5,9},{9,13},{13,1},{2,6},{6,10},{... | collective-permute-start | bytes 430088 | tf_op jit(solution)/shard_map/ppermute | solution.py:26
  15.7 10.2 %collective-permute-start.4 = (f32[10,3584]{1,0:T(8,128)S(1)}, f32[10,3584]{1,0:T(8,128)S(1)}, u32[]{:S(2)}, u32[]{:S(2)}) collective-permute-start(f32[10,3584]{1,0:T(8,128)S(1)} %get-tuple-element.20.here), channel_id=1, source_target_pairs={{0,12},{4,0},{8,4},{12,8},{1,13},{5,1},{9,5},{13,9},{2,14},{6,2},{... | collective-permute-start | bytes 430088 | tf_op jit(solution)/shard_map/ppermute | solution.py:26
  18.8 8.9 %collective-permute-start.5 = (f32[10,512]{1,0:T(8,128)S(1)}, f32[10,512]{1,0:T(8,128)S(1)}, u32[]{:S(2)}, u32[]{:S(2)}) collective-permute-start(f32[10,512]{1,0:T(8,128)S(1)} %pad_maximum_fusion), channel_id=1, source_target_pairs={{0,8},{4,12},{8,0},{12,4},{1,9},{5,13},{9,1},{13,5},{2,10},{6,14},... | collective-permute-start | bytes 61448 | tf_op jit(solution)/shard_map/ppermute | solution.py:26
  23.9 8.6 %copy-start.1 = (f32[10,3584]{1,0:T(8,128)}, f32[10,3584]{1,0:T(8,128)S(1)}, u32[]{:S(2)}) copy-start(f32[10,3584]{1,0:T(8,128)S(1)} %collective-permute-done.3.below) | copy-start | bytes 430084
  25.9 6.6 %copy-start.2 = (f32[10,3584]{1,0:T(8,128)}, f32[10,3584]{1,0:T(8,128)S(1)}, u32[]{:S(2)}) copy-start(f32[10,3584]{1,0:T(8,128)S(1)} %collective-permute-done.4.above) | copy-start | bytes 430084
  27.7 0.7 %copy-start.3 = (f32[10,2048]{1,0:T(8,128)}, f32[10,2048]{1,0:T(8,128)S(1)}, u32[]{:S(2)}) copy-start(f32[10,2048]{1,0:T(8,128)S(1)} %constant_dynamic-update-slice_fusion.4.values) | copy-start | bytes 245764
